TPU v7x, 32 devices: a whole 2x2x4 slice. The times are simulated.
32 devices in a mesh: batch: 8 (over z, x), head: 4 (over y, core).
Axes of the slice: x: 2, y: 2, z: 4, core: 2. Of those that a mesh axis runs over, the one named last changes fastest.
Arguments:
- tokens: bfloat16 [4096, 2048], P('batch', 'head'), may hold values from -96 to 96
- lengths: int32 [32], P('batch'), may hold values from 1 to 128
- states: float32 [32, 16, 128, 128], P('batch', 'head'), may hold values from -3 to 3
- norm_gain: float32 [2048], replicated, may hold values from 0.1 to 1.9
- mix_weight: bfloat16 [2048, 14336], P(None, 'head'), may hold values from -0.125 to 0.125
- rate_weight: bfloat16 [2048, 64], P(None, 'head'), may hold values from -0.5524272 to 0.5524272
- decay_rate: float32 [16], P('head'), may hold values from 0.0005 to 0.03
- head_gain: float32 [128], replicated, may hold values from 0.1 to 1.9
- out_weight: bfloat16 [2048, 2048], P('head'), may hold values from -0.125 to 0.125
- final_gain: float32 [2048], replicated, may hold values from 0.1 to 1.9
- vocab_table: bfloat16 [16384, 2048], P(('batch', 'head')), may hold values from -50.8233 to 50.8233
- next_token: int32 [32], replicated, may hold values from 0 to 16383
Outputs:
- mixed: bfloat16 [4096, 2048], P('batch', 'head')
- new_state: float32 [32, 16, 128, 128], P('batch', 'head')
- log_likelihood: float32 [32], replicated
All inputs are finite; a program needn't handle non-finite values.
Results may differ from a plain program's by a relative error of at most 0.0058.
The roundings to bfloat16 on the way count: a program that leaves them out, or rounds other values in their place, can miss the bound.
Values may be sent and summed in bfloat16 or wider, within the bound.
No kernel may reach another device: no remote copies, remote signals or barrier semaphores. Data moves between devices by JAX's collectives and lax.ppermute only.
A program may use at most 128 MiB of HBM per device.

v0:
```python
import jax
import jax.numpy as jnp
from jax import lax
from jax.experimental import pallas as pl
from jax.experimental.pallas import tpu as pltpu
from jax.sharding import PartitionSpec as P


HEAD_DIM = 128
REFLECT = 3
NEW_POSITIONS = 128
CHUNK = 32
BASE = 8
GROUP = 2
STEPS = CHUNK * REFLECT
BLOCKS = 2 * REFLECT + 1

ROW_EPSILON = 1e-05
KEY_EPSILON = 1e-06


NN = (((1,), (0,)), ((), ()))
NT = (((1,), (1,)), ((), ()))
TN = (((0,), (0,)), ((), ()))


def halves(a):
    high = a.astype(jnp.bfloat16)
    return high, (a - high.astype(jnp.float32)).astype(jnp.bfloat16)


def dot1(a, b, dims=NN):
    return lax.dot_general(
        a.astype(jnp.bfloat16), b.astype(jnp.bfloat16), dims, preferred_element_type=jnp.float32
    )


def dot3(a, b, dims=NN):
    ah, al = halves(a)
    bh, bl = halves(b)
    cross = dot1(ah, bl, dims) + dot1(al, bh, dims)
    return dot1(ah, bh, dims) + cross


def silu(x):
    return x / (1.0 + jnp.exp(-x))


def interleave(parts):
    pieces = []
    for b in range(CHUNK // BASE):
        for part in parts:
            pieces.append(part[b * BASE : (b + 1) * BASE])
    return jnp.concatenate(pieces, axis=0)


def position_of(r):
    b = jnp.zeros_like(r)
    for n in range(1, CHUNK // BASE):
        b = b + (r >= n * BASE * REFLECT).astype(jnp.int32)
    rest = r - b * (BASE * REFLECT)
    j = jnp.zeros_like(r)
    for n in range(1, REFLECT):
        j = j + (rest >= n * BASE).astype(jnp.int32)
    return b * BASE + rest - j * BASE, j


def mixer_kernel(head_count, *refs):
    index_ref, lengths_ref, rate_ref = refs[:3]
    token_refs = refs[3 : 3 + head_count]
    (gain_ref, mix_ref, rate_weight_ref, head_gain_ref, state_ref) = refs[
        3 + head_count : 8 + head_count
    ]
    normed_ref, new_state_ref = refs[8 + head_count : 10 + head_count]
    (scaled_ref, inverse_ref, rates_ref, projected_ref) = refs[10 + head_count : 14 + head_count]
    (fresh_ref, reads_ref, scores_ref, tails_ref, decays_ref) = refs[14 + head_count :]
    h = pl.program_id(0)
    width = token_refs[0].shape[1]
    sequences = state_ref.shape[0]

    @pl.when(h == 0)
    def _():
        squares = 0.0
        for k in range(head_count):
            at = pl.multiple_of((index_ref[0] ^ k) * width, width)
            wide = token_refs[k][...].astype(jnp.float32)
            squares = squares + jnp.sum(wide * wide, axis=1, keepdims=True)
            scaled_ref[:, pl.ds(at, width)] = (wide * gain_ref[:, pl.ds(at, width)]).astype(
                jnp.bfloat16
            )
        inverse = lax.rsqrt(squares / (width * head_count) + ROW_EPSILON)
        inverse_ref[...] = inverse
        rates_ref[...] = (
            jnp.dot(scaled_ref[...], rate_weight_ref[...], preferred_element_type=jnp.float32)
            * inverse
        )

    projected_ref[...] = (
        jnp.dot(scaled_ref[...], mix_ref[...], preferred_element_type=jnp.float32)
        * inverse_ref[...]
    )
    new_state_ref[...] = state_ref[...]
    decay_rate = rate_ref[h]

    def prepare(g, carry):
        square = (STEPS, STEPS)
        p_r, j_r = position_of(lax.broadcasted_iota(jnp.int32, square, 0))
        p_c, j_c = position_of(lax.broadcasted_iota(jnp.int32, square, 1))
        same = p_r == p_c
        eye = same & (j_r == j_c)
        strict = (p_r > p_c) | (same & (j_r > j_c))
        up_to = p_r <= p_c
        q_pos = lax.broadcasted_iota(jnp.int32, (CHUNK, STEPS), 0)
        q_col, q_j = position_of(lax.broadcasted_iota(jnp.int32, (CHUNK, STEPS), 1))
        visible = q_col <= q_pos
        q_pick = (q_col == q_pos) & (q_j == 0)
        identity = jnp.where(eye, 1.0, 0.0)
        chains = [(g * GROUP + n, s) for n in range(GROUP) for s in range(sequences)]
        each = range(len(chains))

        keys, lefts, values, betas, rows, cols, qcums, totals = [], [], [], [], [], [], [], []
        for c, s in chains:
            at = pl.ds(pl.multiple_of(s * NEW_POSITIONS + c * CHUNK, CHUNK), CHUNK)
            block = [
                silu(projected_ref[at, n * HEAD_DIM : (n + 1) * HEAD_DIM]) for n in range(BLOCKS)
            ]
            key_parts = [
                k * lax.rsqrt(jnp.sum(k * k, axis=1, keepdims=True) + KEY_EPSILON)
                for k in block[1 : REFLECT + 1]
            ]
            rates = rates_ref[at, :]
            lane = lax.broadcasted_iota(jnp.int32, rates.shape, 1)
            picked = [
                jnp.sum(
                    jnp.where(lane == h * (REFLECT + 1) + j, rates, 0.0), axis=1, keepdims=True
                )
                for j in range(REFLECT + 1)
            ]
            position = c * CHUNK + lax.broadcasted_iota(jnp.int32, (CHUNK, 1), 0)
            valid = position < lengths_ref[s]
            beta_parts = [
                jnp.where(valid, 2.0 / (1.0 + jnp.exp(-x)), 0.0) for x in picked[:REFLECT]
            ]
            d = picked[REFLECT]
            soft = jnp.maximum(d, 0.0) + jnp.log1p(jnp.exp(-jnp.abs(d)))
            log_decay = jnp.where(valid, -decay_rate * soft, 0.0)
            zero = jnp.zeros_like(log_decay)
            step_decay = interleave([log_decay] + [zero] * (REFLECT - 1))
            row = jnp.sum(jnp.where(up_to, step_decay, 0.0), axis=0, keepdims=True)
            key = interleave(key_parts)
            keys.append(key)
            lefts.append(jnp.concatenate([key, block[0]], axis=0))
            values.append(interleave(block[REFLECT + 1 :]))
            betas.append(interleave(beta_parts))
            rows.append(row)
            cols.append(jnp.sum(jnp.where(eye, row, 0.0), axis=1, keepdims=True))
            qcums.append(jnp.sum(jnp.where(q_pick, row, 0.0), axis=1, keepdims=True))
            totals.append(jnp.sum(log_decay, axis=0, keepdims=True))

        grams = [dot3(lefts[s], keys[s], NT) for s in each]
        lower = [
            betas[s]
            * jnp.exp(jnp.where(strict, cols[s] - rows[s], -jnp.inf))
            * grams[s][:STEPS]
            for s in each
        ]
        scores = [
            grams[s][STEPS:] * jnp.exp(jnp.where(visible, qcums[s] - rows[s], -jnp.inf))
            for s in each
        ]
        inner = [jnp.where(same, a, 0.0) for a in lower]
        inverses = [identity - d + dot1(d, d) for d in inner]
        level = 1
        while level < CHUNK:
            pair = ((p_r ^ p_c) < 2 * level) & ((p_r ^ p_c) >= level)
            off = [jnp.where(pair, a, 0.0) for a in lower]
            left = [dot1(inverses[s], off[s]) for s in each]
            inverses = [inverses[s] - dot1(left[s], inverses[s]) for s in each]
            level *= 2
        right = [
            jnp.concatenate([betas[n] * values[n], betas[n] * jnp.exp(cols[n]) * keys[n]], axis=1)
            for n in each
        ]
        solved = [dot1(inverses[n], right[n]) for n in each]
        residuals = [right[n] - solved[n] - dot3(lower[n], solved[n]) for n in each]
        solved = [solved[n] + dot1(inverses[n], residuals[n]) for n in each]
        for n in each:
            c, s = chains[n]
            slot = c * sequences + s
            fresh_ref[slot] = solved[n][:, :HEAD_DIM]
            reads_ref[slot, :STEPS] = solved[n][:, HEAD_DIM:]
            reads_ref[slot, STEPS:] = jnp.exp(qcums[n]) * lefts[n][STEPS:]
            scores_ref[slot] = scores[n]
            tails_ref[slot] = jnp.exp(totals[n] - cols[n]) * keys[n]
            decays_ref[slot] = jnp.broadcast_to(jnp.exp(totals[n]), (8, HEAD_DIM))
        return carry

    lax.fori_loop(0, NEW_POSITIONS // (CHUNK * GROUP), prepare, 0)

    def advance(c, carry):
        each = range(sequences)
        slots = [c * sequences + s for s in each]
        images = [dot3(reads_ref[slots[s]], new_state_ref[s, 0], NT) for s in each]
        updates = [fresh_ref[slots[s]] - images[s][:STEPS] for s in each]
        for s in each:
            new_state_ref[s, 0] = decays_ref[slots[s], 0:1, :] * new_state_ref[s, 0] + dot3(
                updates[s], tails_ref[slots[s]], TN
            )
        for s in each:
            o = images[s][STEPS:] + dot3(scores_ref[slots[s]], updates[s])
            factor = lax.rsqrt(jnp.mean(o * o, axis=1, keepdims=True) + ROW_EPSILON)
            at = pl.multiple_of(s * NEW_POSITIONS + c * CHUNK, CHUNK)
            normed_ref[pl.ds(at, CHUNK), :] = (o * factor * head_gain_ref[...]).astype(
                jnp.bfloat16
            )
        return carry

    lax.fori_loop(0, NEW_POSITIONS // CHUNK, advance, 0)


def mixer(index, lengths, decay_rate, blocks, norm_gain, mix_weight, rate_weight, head_gain, states):
    rows, width = blocks[0].shape
    head_count = len(blocks)
    model_width = norm_gain.shape[0]
    sequences, local_heads = states.shape[:2]
    columns = BLOCKS * HEAD_DIM
    slots = sequences * NEW_POSITIONS // CHUNK
    smem = pl.BlockSpec(memory_space=pltpu.SMEM)

    def whole(shape):
        return pl.BlockSpec(shape, lambda h: (0,) * len(shape))

    state_spec = pl.BlockSpec(
        (sequences, 1, HEAD_DIM, HEAD_DIM), lambda h: (0, h, 0, 0)
    )
    return pl.pallas_call(
        lambda *refs: mixer_kernel(head_count, *refs),
        grid=(local_heads,),
        in_specs=[smem, smem, smem]
        + [whole((rows, width))] * head_count
        + [
            whole((1, model_width)),
            pl.BlockSpec((model_width, columns), lambda h: (0, h)),
            whole(rate_weight.shape),
            whole((1, HEAD_DIM)),
            state_spec,
        ],
        out_specs=[pl.BlockSpec((rows, HEAD_DIM), lambda h: (0, h)), state_spec],
        out_shape=[
            jax.ShapeDtypeStruct((rows, local_heads * HEAD_DIM), jnp.bfloat16),
            jax.ShapeDtypeStruct(states.shape, jnp.float32),
        ],
        scratch_shapes=[
            pltpu.VMEM((rows, model_width), jnp.bfloat16),
            pltpu.VMEM((rows, 1), jnp.float32),
            pltpu.VMEM((rows, rate_weight.shape[1]), jnp.float32),
            pltpu.VMEM((rows, columns), jnp.float32),
            pltpu.VMEM((slots, STEPS, HEAD_DIM), jnp.float32),
            pltpu.VMEM((slots, STEPS + CHUNK, HEAD_DIM), jnp.float32),
            pltpu.VMEM((slots, CHUNK, STEPS), jnp.float32),
            pltpu.VMEM((slots, STEPS, HEAD_DIM), jnp.float32),
            pltpu.VMEM((slots, 8, HEAD_DIM), jnp.float32),
        ],
        cost_estimate=pl.CostEstimate(
            flops=24 * rows * model_width * columns,
            bytes_accessed=2 * model_width * columns * local_heads,
            transcendentals=0,
        ),
        compiler_params=pltpu.CompilerParams(
            dimension_semantics=("arbitrary",), vmem_limit_bytes=48 * 1024 * 1024
        ),
        name="mixer",
    )(
        index,
        lengths,
        decay_rate,
        *blocks,
        norm_gain[None, :],
        mix_weight,
        rate_weight,
        head_gain[None, :],
        states,
    )


def project_kernel(head_count, *refs):
    lengths_ref = refs[0]
    normed_refs = refs[1 : 1 + head_count]
    weight_refs = refs[1 + head_count : 1 + 2 * head_count]
    tokens_ref, mixed_ref, last_ref, rounded_ref = refs[1 + 2 * head_count :]
    total = jnp.dot(normed_refs[0][...], weight_refs[0][...], preferred_element_type=jnp.float32)
    for k in range(1, head_count):
        total = total + jnp.dot(
            normed_refs[k][...], weight_refs[k][...], preferred_element_type=jnp.float32
        )
    mixed = (tokens_ref[...].astype(jnp.float32) + total).astype(jnp.bfloat16)
    mixed_ref[...] = mixed
    rounded_ref[...] = mixed.astype(jnp.float32)
    for s in range(last_ref.shape[0]):
        at = s * NEW_POSITIONS + lengths_ref[s] - 1
        last_ref[pl.ds(s, 1), :] = rounded_ref[pl.ds(at, 1), :]


def project(lengths, normed_blocks, weight_blocks, tokens):
    head_count = len(normed_blocks)
    vmem = pl.BlockSpec(memory_space=pltpu.VMEM)
    return pl.pallas_call(
        lambda *refs: project_kernel(head_count, *refs),
        in_specs=[pl.BlockSpec(memory_space=pltpu.SMEM)] + [vmem] * (2 * head_count + 1),
        out_specs=[vmem, vmem],
        out_shape=[
            jax.ShapeDtypeStruct(tokens.shape, jnp.bfloat16),
            jax.ShapeDtypeStruct((lengths.shape[0], tokens.shape[1]), jnp.float32),
        ],
        scratch_shapes=[pltpu.VMEM(tokens.shape, jnp.float32)],
        compiler_params=pltpu.CompilerParams(vmem_limit_bytes=48 * 1024 * 1024),
        name="project",
    )(lengths, *normed_blocks, *weight_blocks, tokens)


def swap(array, axis, k):
    size = lax.axis_size(axis)
    return lax.ppermute(array, axis, [(i, i ^ k) for i in range(size)])


def spread(array, axis):
    blocks = {0: array}
    bit = lax.axis_size(axis) // 2
    while bit >= 1:
        for k in list(blocks):
            blocks[k ^ bit] = swap(blocks[k], axis, bit)
        bit //= 2
    return [blocks[k] for k in range(len(blocks))]


def score_kernel(batch_count, head_count, *refs):
    index_ref, next_ref, gain_ref, table_ref = refs[:4]
    row_refs = refs[4 : 4 + batch_count]
    stats_ref, everyone_ref = refs[4 + batch_count :]
    sequences, model_width = row_refs[0].shape
    width = model_width // head_count
    for m in range(batch_count):
        rows = row_refs[m][...].astype(jnp.float32)
        at = (index_ref[0] ^ m) * sequences
        for k in range(head_count):
            to = pl.multiple_of((index_ref[1] ^ k) * width, width)
            for r in range(sequences):
                everyone_ref[pl.ds(at + r, 1), pl.ds(to, width)] = rows[
                    r : r + 1, k * width : (k + 1) * width
                ]
    wide = everyone_ref[...]
    factor = lax.rsqrt(jnp.mean(wide * wide, axis=1, keepdims=True) + ROW_EPSILON)
    hidden = (wide * factor * gain_ref[...]).astype(jnp.bfloat16)
    logits = lax.dot_general(hidden, table_ref[...], NT, preferred_element_type=jnp.float32)
    ids = index_ref[2] + lax.broadcasted_iota(jnp.int32, logits.shape, 1)
    largest = jnp.max(logits, axis=1, keepdims=True)
    total = jnp.sum(jnp.exp(logits - largest), axis=1, keepdims=True)
    target = jnp.sum(jnp.where(ids == next_ref[...], logits, 0.0), axis=1, keepdims=True)
    lane = lax.broadcasted_iota(jnp.int32, stats_ref.shape, 1)
    stats_ref[...] = jnp.where(lane == 0, largest, jnp.where(lane == 1, total, target))


def score(index, next_token, final_gain, vocab_table, rows, head_count):
    everyone = (len(rows) * rows[0].shape[0], rows[0].shape[1])
    vmem = pl.BlockSpec(memory_space=pltpu.VMEM)
    return pl.pallas_call(
        lambda *refs: score_kernel(len(rows), head_count, *refs),
        in_specs=[pl.BlockSpec(memory_space=pltpu.SMEM)] + [vmem] * (3 + len(rows)),
        out_specs=vmem,
        out_shape=jax.ShapeDtypeStruct((everyone[0], HEAD_DIM), jnp.float32),
        scratch_shapes=[pltpu.VMEM(everyone, jnp.float32)],
        name="score",
    )(index, next_token[:, None], final_gain[None, :], vocab_table, *rows)


def combine_kernel(finish, index_ref, *refs):
    part_refs, out_ref, all_ref = refs[:-2], refs[-2], refs[-1]
    count = len(part_refs)
    for k in range(count):
        all_ref[index_ref[0] ^ k] = part_refs[k][...]
    parts = [all_ref[k] for k in range(count)]
    largest = parts[0][:, 0:1]
    for part in parts[1:]:
        largest = jnp.maximum(largest, part[:, 0:1])
    total, target = 0.0, 0.0
    for part in parts:
        total = total + part[:, 1:2] * jnp.exp(part[:, 0:1] - largest)
        target = target + part[:, 2:3]
    if finish:
        out_ref[...] = jnp.broadcast_to(target - (largest + jnp.log(total)), out_ref.shape)
    else:
        lane = lax.broadcasted_iota(jnp.int32, out_ref.shape, 1)
        out_ref[...] = jnp.where(lane == 0, largest, jnp.where(lane == 1, total, target))


def combine(index, parts, finish):
    vmem = pl.BlockSpec(memory_space=pltpu.VMEM)
    return pl.pallas_call(
        lambda *refs: combine_kernel(finish, *refs),
        in_specs=[pl.BlockSpec(memory_space=pltpu.SMEM)] + [vmem] * len(parts),
        out_specs=vmem,
        out_shape=jax.ShapeDtypeStruct(parts[0].shape, jnp.float32),
        scratch_shapes=[pltpu.VMEM((len(parts),) + parts[0].shape, jnp.float32)],
        name="combine",
    )(index, *parts)


def direct(array, axis):
    return [array] + [swap(array, axis, k) for k in range(1, lax.axis_size(axis))]


def on_device(
    tokens,
    lengths,
    states,
    norm_gain,
    mix_weight,
    rate_weight,
    decay_rate,
    head_gain,
    out_weight,
    final_gain,
    vocab_table,
    next_token,
):
    local_width = tokens.shape[1]
    head_count = lax.axis_size("head")
    index = lax.axis_index("head")
    token_blocks = spread(tokens, "head")

    held = lax.optimization_barrier((out_weight, *token_blocks))
    early_weight, token_blocks = held[0], list(held[1:])
    weight_blocks = []
    for k in range(head_count):
        piece = lax.dynamic_slice(
            early_weight, (0, (index ^ k) * local_width), (out_weight.shape[0], local_width)
        )
        weight_blocks.append(swap(piece, "head", k) if k else piece)

    normed, new_state = mixer(
        index[None].astype(jnp.int32),
        lengths,
        decay_rate,
        token_blocks,
        norm_gain,
        mix_weight,
        rate_weight,
        head_gain,
        states,
    )
    mixed, last_rows = project(lengths, spread(normed, "head"), weight_blocks, tokens)
    last_rows = last_rows.astype(jnp.bfloat16)

    batch_index = lax.axis_index("batch").astype(jnp.int32)
    head_index = index.astype(jnp.int32)
    vocab_start = (batch_index * head_count + head_index) * vocab_table.shape[0]
    joined = jnp.concatenate(direct(last_rows, "head"), axis=1)
    stats = score(
        jnp.stack([batch_index, head_index, vocab_start]),
        next_token,
        final_gain,
        vocab_table,
        direct(joined, "batch"),
        head_count,
    )
    stats = combine(head_index[None], direct(stats, "head"), False)
    scored = combine(batch_index[None], direct(stats, "batch"), True)
    return (mixed, new_state, scored[:, 0])


def solution(mesh):
    placed = (
        P("batch", "head"),
        P("batch"),
        P("batch", "head", None, None),
        P(),
        P(None, "head"),
        P(None, "head"),
        P("head"),
        P(),
        P("head", None),
        P(),
        P(("batch", "head"), None),
        P(),
    )
    return jax.shard_map(
        on_device,
        mesh=mesh,
        in_specs=placed,
        out_specs=(P("batch", "head"), P("batch", "head", None, None), P()),
        check_vma=False,
    )
```

profile of v0, /device:TPU:0, one launch (start us, length us, event | category | flops | bytes accessed | tf_op | source)
XLA Modules:
  0.0 160.9 jit_solution(14788912880659029925)
XLA Ops:
  0.6 3.1 %collective-permute-start.1 = (bf16[512,512]{1,0:T(8,128)(2,1)}, bf16[512,512]{1,0:T(8,128)(2,1)S(1)}, u32[]{:S(2)}, u32[]{:S(2)}) collective-permute-start(bf16[512,512]{1,0:T(8,128)(2,1)} %refs_9_.2), channel_id=1, source_target_pairs={{0,2},{1,3},{2,0},{3,1},{4,6},{5,7},{6,4},{7,5},{8,10},{9,11},{10,... | collective-permute-start | bytes 1572872 | tf_op jit(solution)/shard_map/ppermute | solution.py:323
  3.7 0.0 collective-permute-start
  3.7 12.1 %collective-permute-done.1.refs_5_ = bf16[512,512]{1,0:T(8,128)(2,1)S(1)} collective-permute-done((bf16[512,512]{1,0:T(8,128)(2,1)}, bf16[512,512]{1,0:T(8,128)(2,1)S(1)}, u32[]{:S(2)}, u32[]{:S(2)}) %collective-permute-start.1) | collective-permute-done | bytes 524320 | tf_op jit(solution)/shard_map/ppermute | solution.py:323
  15.8 0.0 collective-permute-start.2
  15.8 1.1 copy.17.refs_9_
  16.9 0.0 collective-permute-done.refs_4_
  17.0 0.8 collective-permute-done.2.refs_6_
  17.7 1.0 copy-done
  18.8 0.7 copy-done.2
  19.4 1.2 copy-done.4
  20.7 0.7 copy-done.5
  21.4 0.7 copy-done.6
  22.0 0.7 copy-done.7
  22.7 49.8 %mixer.1 = (bf16[512,512]{1,0:T(8,128)(2,1)S(1)}, f32[4,4,128,128]{3,2,1,0:T(8,128)}) custom-call(s32[1]{0:T(128)} %bitcast.refs_0_, s32[4]{0:T(128)S(1)} %copy-done.2, f32[4]{0:T(128)S(1)} %copy-done.6, bf16[512,512]{1,0:T(8,128)(2,1)S(1)} %copy-done, bf16[512,512]{1,0:T(8,128)(2,1)S(1)} %collective-permute-done.refs_4_, ...), custom_call_target="tpu_custom_call" | custom-call | flops 22548578304 | bytes 14680064 | tf_op jit(solution)/shard_map/mixer/pallas_call | solution.py:236
  72.4 1.7 %collective-permute-start.4 = (bf16[512,512]{1,0:T(8,128)(2,1)S(1)}, bf16[512,512]{1,0:T(8,128)(2,1)S(1)}, u32[]{:S(2)}, u32[]{:S(2)}) collective-permute-start(bf16[512,512]{1,0:T(8,128)(2,1)S(1)} %get-tuple-element.16.refs_1_), channel_id=1, source_target_pairs={{0,2},{1,3},{2,0},{3,1},{4,6},{5,7},{6,4},{7,5},{8,10},{9,11},{10,... | collective-permute-start | bytes 1572872 | tf_op jit(solution)/shard_map/ppermute | solution.py:323
  74.2 0.0 collective-permute-start.3
  74.2 1.7 %constant_dynamic-slice_fusion = (bf16[512,512]{1,0:T(8,128)(2,1)S(1)}, bf16[512,512]{1,0:T(8,128)(2,1)S(1)}, bf16[512,512]{1,0:T(8,128)(2,1)S(1)}, bf16[512,512]{1,0:T(8,128)(2,1)S(1)}) fusion(bf16[512,2048]{1,0:T(8,128)(2,1)} %param.20, s32[]{:T(128)S(6)} %select_n.15, s32[]{:T(128)S(6)} %select_n.14, s32[]{:T(128)S(6)} %select_n.13, s32[]{:T(128)S(6)} %select_n.12), kind=kLoop, calls=%fused_computation.2 | loop fusion | bytes 4194320 | tf_op jit(solution)/shard_map/dynamic_slice | solution.py:435
  75.9 0.5 collective-permute-start.6
  76.4 0.3 collective-permute-start.7
  76.7 1.1 collective-permute-start.8
  77.9 9.4 %collective-permute-done.4.refs_3_ = bf16[512,512]{1,0:T(8,128)(2,1)S(1)} collective-permute-done((bf16[512,512]{1,0:T(8,128)(2,1)S(1)}, bf16[512,512]{1,0:T(8,128)(2,1)S(1)}, u32[]{:S(2)}, u32[]{:S(2)}) %collective-permute-start.4) | collective-permute-done | bytes 524320 | tf_op jit(solution)/shard_map/ppermute | solution.py:323
  87.2 0.0 collective-permute-done.6.refs_6_
  87.2 11.2 %collective-permute-done.7.refs_7_ = bf16[512,512]{1,0:T(8,128)(2,1)S(1)} collective-permute-done((bf16[512,512]{1,0:T(8,128)(2,1)S(1)}, bf16[512,512]{1,0:T(8,128)(2,1)S(1)}, u32[]{:S(2)}, u32[]{:S(2)}) %collective-permute-start.7) | collective-permute-done | bytes 524320 | tf_op jit(solution)/shard_map/ppermute | solution.py:323
  98.5 9.7 %collective-permute-done.8.refs_8_ = bf16[512,512]{1,0:T(8,128)(2,1)S(1)} collective-permute-done((bf16[512,512]{1,0:T(8,128)(2,1)S(1)}, bf16[512,512]{1,0:T(8,128)(2,1)S(1)}, u32[]{:S(2)}, u32[]{:S(2)}) %collective-permute-start.8) | collective-permute-done | bytes 524320 | tf_op jit(solution)/shard_map/ppermute | solution.py:323
  108.1 0.0 collective-permute-done.3.refs_2_
  108.1 0.0 collective-permute-done.5.refs_4_
  108.2 0.0 copy-start.26
  108.2 2.6 %project.1 = (bf16[512,512]{1,0:T(8,128)(2,1)}, f32[4,512]{1,0:T(4,128)S(1)}) custom-call(s32[4]{0:T(128)S(1)} %copy-done.3, bf16[512,512]{1,0:T(8,128)(2,1)S(1)} %get-tuple-element.16.refs_1_, bf16[512,512]{1,0:T(8,128)(2,1)S(1)} %collective-permute-done.3.refs_2_, bf16[512,512]{1,0:T(8,128)(2,1)S(1)} %collective-permute-done.4.refs_3_, ...), custom_call_target="tpu_custom_call" | custom-call | tf_op jit(solution)/shard_map/project/pallas_call | solution.py:307
  110.8 1.6 %collective-permute-start.10 = (bf16[4,512]{1,0:T(4,128)(2,1)S(1)}, bf16[4,512]{1,0:T(4,128)(2,1)S(1)}, u32[]{:S(2)}, u32[]{:S(2)}) collective-permute-start(bf16[4,512]{1,0:T(4,128)(2,1)S(1)} %convert_element_type.3), channel_id=1, source_target_pairs={{0,2},{1,3},{2,0},{3,1},{4,6},{5,7},{6,4},{7,5},{8,10},{9,11},{10,... | collective-permute-start | bytes 12296 | tf_op jit(solution)/shard_map/ppermute | solution.py:323
  112.4 0.3 collective-permute-start.11
  112.7 0.2 collective-permute-start.9
  112.9 1.5 collective-permute-done.10
  114.4 1.1 collective-permute-done.11
  115.4 0.0 collective-permute-done.9
  115.5 1.6 collective-permute-start.12
  117.0 1.6 collective-permute-start.13
  118.6 0.4 collective-permute-start.14
  119.0 2.6 %collective-permute-start.15 = (bf16[4,2048]{1,0:T(4,128)(2,1)S(1)}, bf16[4,2048]{1,0:T(4,128)(2,1)S(1)}, u32[]{:S(2)}, u32[]{:S(2)}) collective-permute-start(bf16[4,2048]{1,0:T(4,128)(2,1)S(1)} %pad_maximum_fusion.refs_4_), channel_id=1, source_target_pairs={{0,16},{4,20},{8,24},{12,28},{16,0},{20,4},{24,8},{28,12},{1,17},{... | collective-permute-start | bytes 49160 | tf_op jit(solution)/shard_map/ppermute | solution.py:323
  121.6 1.3 collective-permute-start.16
  122.9 3.6 %collective-permute-start.17 = (bf16[4,2048]{1,0:T(4,128)(2,1)S(1)}, bf16[4,2048]{1,0:T(4,128)(2,1)S(1)}, u32[]{:S(2)}, u32[]{:S(2)}) collective-permute-start(bf16[4,2048]{1,0:T(4,128)(2,1)S(1)} %pad_maximum_fusion.refs_4_), channel_id=1, source_target_pairs={{0,24},{4,28},{8,16},{12,20},{16,8},{20,12},{24,0},{28,4},{1,25},{... | collective-permute-start | bytes 49160 | tf_op jit(solution)/shard_map/ppermute | solution.py:323
  126.5 0.2 collective-permute-start.18
  126.7 0.6 pad_add_fusion.refs_0_
  127.2 0.7 copy.18.refs_1_
  128.0 0.4 collective-permute-done.17.refs_10_
  128.4 4.5 %collective-permute-done.18.refs_11_ = bf16[4,2048]{1,0:T(4,128)(2,1)S(1)} collective-permute-done((bf16[4,2048]{1,0:T(4,128)(2,1)S(1)}, bf16[4,2048]{1,0:T(4,128)(2,1)S(1)}, u32[]{:S(2)}, u32[]{:S(2)}) %collective-permute-start.18) | collective-permute-done | bytes 16416 | tf_op jit(solution)/shard_map/ppermute | solution.py:323
  133.0 0.5 copy-done.15
  133.5 3.5 %score.1.refs_1_ = f32[32,128]{1,0:T(8,128)} custom-call(s32[3]{0:T(128)} %pad_add_fusion.refs_0_, s32[32,1]{1,0:T(8,128)} %copy.18.refs_1_, f32[1,2048]{1,0:T(1,128)} %bitcast.9, bf16[512,2048]{1,0:T(8,128)(2,1)} %refs_3_.2, bf16[4,2048]{1,0:T(4,128)(2,1)} %copy-done.8, bf16[4,2048]{1,0:T(4,128)(2,1)} %copy-done.9, bf16[4,2048]{1,0:T(4,128)(2,1)} %copy-done.10, ...), custom_call_target="tpu_custom_call" | custom-call | tf_op jit(solution)/shard_map/score/pallas_call | solution.py:366
  137.0 0.6 collective-permute-start.20
  137.5 1.3 collective-permute-start.21
  138.8 2.3 %collective-permute-done.20.refs_3_ = f32[32,128]{1,0:T(8,128)S(1)} collective-permute-done((f32[32,128]{1,0:T(8,128)}, f32[32,128]{1,0:T(8,128)S(1)}, u32[]{:S(2)}, u32[]{:S(2)}) %collective-permute-start.20) | collective-permute-done | bytes 16416 | tf_op jit(solution)/shard_map/ppermute | solution.py:323
  141.1 0.0 collective-permute-done.21.refs_4_
  141.1 0.6 copy-done.24
  141.7 0.6 copy-done.25
  142.3 1.5 combine.2.refs_1_
  143.8 0.6 collective-permute-start.22
  144.4 2.9 %collective-permute-start.24 = (f32[32,128]{1,0:T(8,128)}, f32[32,128]{1,0:T(8,128)S(1)}, u32[]{:S(2)}, u32[]{:S(2)}) collective-permute-start(f32[32,128]{1,0:T(8,128)} %combine.2.refs_1_), channel_id=1, source_target_pairs={{0,12},{4,8},{8,4},{12,0},{16,28},{20,24},{24,20},{28,16},{1,13},{... | collective-permute-start | bytes 49160 | tf_op jit(solution)/shard_map/ppermute | solution.py:323
  147.3 2.9 %collective-permute-start.26 = (f32[32,128]{1,0:T(8,128)}, f32[32,128]{1,0:T(8,128)S(1)}, u32[]{:S(2)}, u32[]{:S(2)}) collective-permute-start(f32[32,128]{1,0:T(8,128)} %combine.2.refs_1_), channel_id=1, source_target_pairs={{0,20},{4,16},{8,28},{12,24},{16,4},{20,0},{24,12},{28,8},{1,21},{... | collective-permute-start | bytes 49160 | tf_op jit(solution)/shard_map/ppermute | solution.py:323
  150.3 0.2 collective-permute-start.27
  150.5 4.5 %collective-permute-start.28 = (f32[32,128]{1,0:T(8,128)}, f32[32,128]{1,0:T(8,128)S(1)}, u32[]{:S(2)}, u32[]{:S(2)}) collective-permute-start(f32[32,128]{1,0:T(8,128)} %combine.2.refs_1_), channel_id=1, source_target_pairs={{0,28},{4,24},{8,20},{12,16},{16,12},{20,8},{24,4},{28,0},{1,29},{... | collective-permute-start | bytes 49160 | tf_op jit(solution)/shard_map/ppermute | solution.py:323
  155.0 1.0 collective-permute-done.27.refs_7_
  156.0 1.1 collective-permute-done.28.refs_8_
  157.2 0.6 copy-done.22
  157.8 1.8 %combine.3 = f32[32,128]{1,0:T(8,128)} custom-call(s32[1]{0:T(128)} %bitcast.3.refs_0_, f32[32,128]{1,0:T(8,128)} %combine.2.refs_1_, f32[32,128]{1,0:T(8,128)} %copy-done.16, f32[32,128]{1,0:T(8,128)} %copy-done.17, f32[32,128]{1,0:T(8,128)} %copy-done.18, f32[32,128]{1,0:T(8,128)} %copy-done.19, f32[32,128]{1,0:T(8,128)} %copy-done.20, ...), custom_call_target="tpu_custom_call" | custom-call | tf_op jit(solution)/shard_map/combine/pallas_call | solution.py:398
  159.5 1.3 slice_reduce_fusion
  (60 shorter events, 0.1 us)
Async XLA Ops:
  0.6 15.2 %collective-permute-start.1 = (bf16[512,512]{1,0:T(8,128)(2,1)}, bf16[512,512]{1,0:T(8,128)(2,1)S(1)}, u32[]{:S(2)}, u32[]{:S(2)}) collective-permute-start(bf16[512,512]{1,0:T(8,128)(2,1)} %refs_9_.2), channel_id=1, source_target_pairs={{0,2},{1,3},{2,0},{3,1},{4,6},{5,7},{6,4},{7,5},{8,10},{9,11},{10,... | collective-permute-start | bytes 1572872 | tf_op jit(solution)/shard_map/ppermute | solution.py:323
  3.7 13.3 %collective-permute-start = (bf16[512,512]{1,0:T(8,128)(2,1)}, bf16[512,512]{1,0:T(8,128)(2,1)S(1)}, u32[]{:S(2)}, u32[]{:S(2)}) collective-permute-start(bf16[512,512]{1,0:T(8,128)(2,1)} %refs_9_.2), channel_id=1, source_target_pairs={{0,1},{1,0},{2,3},{3,2},{4,5},{5,4},{6,7},{7,6},{8,9},{9,8},{10,11... | collective-permute-start | bytes 1572872 | tf_op jit(solution)/shard_map/ppermute | solution.py:323
  15.8 1.9 %collective-permute-start.2 = (bf16[512,512]{1,0:T(8,128)(2,1)S(1)}, bf16[512,512]{1,0:T(8,128)(2,1)S(1)}, u32[]{:S(2)}, u32[]{:S(2)}) collective-permute-start(bf16[512,512]{1,0:T(8,128)(2,1)S(1)} %collective-permute-done.1.refs_5_), channel_id=1, source_target_pairs={{0,1},{1,0},{2,3},{3,2},{4,5},{5,4},{6,7},{7,6},{8,9},{9,8},{10,11... | collective-permute-start | bytes 1572872 | tf_op jit(solution)/shard_map/ppermute | solution.py:323
  17.7 1.0 copy-start
  18.8 0.7 copy-start.2
  19.4 1.2 copy-start.4
  20.7 0.7 copy-start.5
  21.4 0.7 copy-start.6
  22.0 0.7 copy-start.7
  72.4 14.8 %collective-permute-start.4 = (bf16[512,512]{1,0:T(8,128)(2,1)S(1)}, bf16[512,512]{1,0:T(8,128)(2,1)S(1)}, u32[]{:S(2)}, u32[]{:S(2)}) collective-permute-start(bf16[512,512]{1,0:T(8,128)(2,1)S(1)} %get-tuple-element.16.refs_1_), channel_id=1, source_target_pairs={{0,2},{1,3},{2,0},{3,1},{4,6},{5,7},{6,4},{7,5},{8,10},{9,11},{10,... | collective-permute-start | bytes 1572872 | tf_op jit(solution)/shard_map/ppermute | solution.py:323
  74.2 34.0 %copy-start.1 = (bf16[512,512]{1,0:T(8,128)(2,1)S(1)}, bf16[512,512]{1,0:T(8,128)(2,1)}, u32[]{:S(2)}) copy-start(bf16[512,512]{1,0:T(8,128)(2,1)} %refs_9_.2) | copy-start | bytes 1572868
  74.2 34.0 %copy-start.3 = (s32[4]{0:T(128)S(1)}, s32[4]{0:T(128)}, u32[]{:S(2)}) copy-start(s32[4]{0:T(128)} %refs_0_.1) | copy-start | bytes 52
  74.2 33.9 %collective-permute-start.3 = (bf16[512,512]{1,0:T(8,128)(2,1)S(1)}, bf16[512,512]{1,0:T(8,128)(2,1)S(1)}, u32[]{:S(2)}, u32[]{:S(2)}) collective-permute-start(bf16[512,512]{1,0:T(8,128)(2,1)S(1)} %get-tuple-element.16.refs_1_), channel_id=1, source_target_pairs={{0,1},{1,0},{2,3},{3,2},{4,5},{5,4},{6,7},{7,6},{8,9},{9,8},{10,11... | collective-permute-start | bytes 1572872 | tf_op jit(solution)/shard_map/ppermute | solution.py:323
  75.9 11.3 %collective-permute-start.6 = (bf16[512,512]{1,0:T(8,128)(2,1)S(1)}, bf16[512,512]{1,0:T(8,128)(2,1)S(1)}, u32[]{:S(2)}, u32[]{:S(2)}) collective-permute-start(bf16[512,512]{1,0:T(8,128)(2,1)S(1)} %get-tuple-element.23), channel_id=1, source_target_pairs={{0,1},{1,0},{2,3},{3,2},{4,5},{5,4},{6,7},{7,6},{8,9},{9,8},{10,11... | collective-permute-start | bytes 1572872 | tf_op jit(solution)/shard_map/ppermute | solution.py:323
  76.4 22.0 %collective-permute-start.7 = (bf16[512,512]{1,0:T(8,128)(2,1)S(1)}, bf16[512,512]{1,0:T(8,128)(2,1)S(1)}, u32[]{:S(2)}, u32[]{:S(2)}) collective-permute-start(bf16[512,512]{1,0:T(8,128)(2,1)S(1)} %get-tuple-element.22), channel_id=1, source_target_pairs={{0,2},{1,3},{2,0},{3,1},{4,6},{5,7},{6,4},{7,5},{8,10},{9,11},{10,... | collective-permute-start | bytes 1572872 | tf_op jit(solution)/shard_map/ppermute | solution.py:323
  76.7 31.4 %collective-permute-start.8 = (bf16[512,512]{1,0:T(8,128)(2,1)S(1)}, bf16[512,512]{1,0:T(8,128)(2,1)S(1)}, u32[]{:S(2)}, u32[]{:S(2)}) collective-permute-start(bf16[512,512]{1,0:T(8,128)(2,1)S(1)} %get-tuple-element.21), channel_id=1, source_target_pairs={{0,3},{1,2},{2,1},{3,0},{4,7},{5,6},{6,5},{7,4},{8,11},{9,10},{10,... | collective-permute-start | bytes 1572872 | tf_op jit(solution)/shard_map/ppermute | solution.py:323
  87.2 20.9 %collective-permute-start.5 = (bf16[512,512]{1,0:T(8,128)(2,1)S(1)}, bf16[512,512]{1,0:T(8,128)(2,1)S(1)}, u32[]{:S(2)}, u32[]{:S(2)}) collective-permute-start(bf16[512,512]{1,0:T(8,128)(2,1)S(1)} %collective-permute-done.4.refs_3_), channel_id=1, source_target_pairs={{0,1},{1,0},{2,3},{3,2},{4,5},{5,4},{6,7},{7,6},{8,9},{9,8},{10,11... | collective-permute-start | bytes 1572872 | tf_op jit(solution)/shard_map/ppermute | solution.py:323
  108.2 19.1 %copy-start.26 = (s32[32]{0:T(128)S(1)}, s32[32]{0:T(128)}, u32[]{:S(2)}) copy-start(s32[32]{0:T(128)} %param.23) | copy-start | bytes 388
  110.8 3.6 %collective-permute-start.10 = (bf16[4,512]{1,0:T(4,128)(2,1)S(1)}, bf16[4,512]{1,0:T(4,128)(2,1)S(1)}, u32[]{:S(2)}, u32[]{:S(2)}) collective-permute-start(bf16[4,512]{1,0:T(4,128)(2,1)S(1)} %convert_element_type.3), channel_id=1, source_target_pairs={{0,2},{1,3},{2,0},{3,1},{4,6},{5,7},{6,4},{7,5},{8,10},{9,11},{10,... | collective-permute-start | bytes 12296 | tf_op jit(solution)/shard_map/ppermute | solution.py:323
  112.4 3.0 %collective-permute-start.11 = (bf16[4,512]{1,0:T(4,128)(2,1)S(1)}, bf16[4,512]{1,0:T(4,128)(2,1)S(1)}, u32[]{:S(2)}, u32[]{:S(2)}) collective-permute-start(bf16[4,512]{1,0:T(4,128)(2,1)S(1)} %convert_element_type.3), channel_id=1, source_target_pairs={{0,3},{1,2},{2,1},{3,0},{4,7},{5,6},{6,5},{7,4},{8,11},{9,10},{10,... | collective-permute-start | bytes 12296 | tf_op jit(solution)/shard_map/ppermute | solution.py:323
  112.7 2.7 %collective-permute-start.9 = (bf16[4,512]{1,0:T(4,128)(2,1)S(1)}, bf16[4,512]{1,0:T(4,128)(2,1)S(1)}, u32[]{:S(2)}, u32[]{:S(2)}) collective-permute-start(bf16[4,512]{1,0:T(4,128)(2,1)S(1)} %convert_element_type.3), channel_id=1, source_target_pairs={{0,1},{1,0},{2,3},{3,2},{4,5},{5,4},{6,7},{7,6},{8,9},{9,8},{10,11... | collective-permute-start | bytes 12296 | tf_op jit(solution)/shard_map/ppermute | solution.py:323
  115.5 17.5 %copy-start.8 = (bf16[4,2048]{1,0:T(4,128)(2,1)}, bf16[4,2048]{1,0:T(4,128)(2,1)S(1)}, u32[]{:S(2)}) copy-start(bf16[4,2048]{1,0:T(4,128)(2,1)S(1)} %pad_maximum_fusion.refs_4_) | copy-start | bytes 49156
  115.5 7.4 %collective-permute-start.12 = (bf16[4,2048]{1,0:T(4,128)(2,1)S(1)}, bf16[4,2048]{1,0:T(4,128)(2,1)S(1)}, u32[]{:S(2)}, u32[]{:S(2)}) collective-permute-start(bf16[4,2048]{1,0:T(4,128)(2,1)S(1)} %pad_maximum_fusion.refs_4_), channel_id=1, source_target_pairs={{0,4},{4,0},{8,12},{12,8},{16,20},{20,16},{24,28},{28,24},{1,5},{5... | collective-permute-start | bytes 49160 | tf_op jit(solution)/shard_map/ppermute | solution.py:323
  117.0 9.4 %collective-permute-start.13 = (bf16[4,2048]{1,0:T(4,128)(2,1)S(1)}, bf16[4,2048]{1,0:T(4,128)(2,1)S(1)}, u32[]{:S(2)}, u32[]{:S(2)}) collective-permute-start(bf16[4,2048]{1,0:T(4,128)(2,1)S(1)} %pad_maximum_fusion.refs_4_), channel_id=1, source_target_pairs={{0,8},{4,12},{8,0},{12,4},{16,24},{20,28},{24,16},{28,20},{1,9},{5... | collective-permute-start | bytes 49160 | tf_op jit(solution)/shard_map/ppermute | solution.py:323
  118.6 9.3 %collective-permute-start.14 = (bf16[4,2048]{1,0:T(4,128)(2,1)S(1)}, bf16[4,2048]{1,0:T(4,128)(2,1)S(1)}, u32[]{:S(2)}, u32[]{:S(2)}) collective-permute-start(bf16[4,2048]{1,0:T(4,128)(2,1)S(1)} %pad_maximum_fusion.refs_4_), channel_id=1, source_target_pairs={{0,12},{4,8},{8,4},{12,0},{16,28},{20,24},{24,20},{28,16},{1,13},{... | collective-permute-start | bytes 49160 | tf_op jit(solution)/shard_map/ppermute | solution.py:323
  119.0 8.9 %collective-permute-start.15 = (bf16[4,2048]{1,0:T(4,128)(2,1)S(1)}, bf16[4,2048]{1,0:T(4,128)(2,1)S(1)}, u32[]{:S(2)}, u32[]{:S(2)}) collective-permute-start(bf16[4,2048]{1,0:T(4,128)(2,1)S(1)} %pad_maximum_fusion.refs_4_), channel_id=1, source_target_pairs={{0,16},{4,20},{8,24},{12,28},{16,0},{20,4},{24,8},{28,12},{1,17},{... | collective-permute-start | bytes 49160 | tf_op jit(solution)/shard_map/ppermute | solution.py:323
  121.6 6.3 %collective-permute-start.16 = (bf16[4,2048]{1,0:T(4,128)(2,1)S(1)}, bf16[4,2048]{1,0:T(4,128)(2,1)S(1)}, u32[]{:S(2)}, u32[]{:S(2)}) collective-permute-start(bf16[4,2048]{1,0:T(4,128)(2,1)S(1)} %pad_maximum_fusion.refs_4_), channel_id=1, source_target_pairs={{0,20},{4,16},{8,28},{12,24},{16,4},{20,0},{24,12},{28,8},{1,21},{... | collective-permute-start | bytes 49160 | tf_op jit(solution)/shard_map/ppermute | solution.py:323
  122.9 10.0 %copy-start.9 = (bf16[4,2048]{1,0:T(4,128)(2,1)}, bf16[4,2048]{1,0:T(4,128)(2,1)S(1)}, u32[]{:S(2)}) copy-start(bf16[4,2048]{1,0:T(4,128)(2,1)S(1)} %collective-permute-done.12.refs_5_) | copy-start | bytes 49156
  122.9 5.5 %collective-permute-start.17 = (bf16[4,2048]{1,0:T(4,128)(2,1)S(1)}, bf16[4,2048]{1,0:T(4,128)(2,1)S(1)}, u32[]{:S(2)}, u32[]{:S(2)}) collective-permute-start(bf16[4,2048]{1,0:T(4,128)(2,1)S(1)} %pad_maximum_fusion.refs_4_), channel_id=1, source_target_pairs={{0,24},{4,28},{8,16},{12,20},{16,8},{20,12},{24,0},{28,4},{1,25},{... | collective-permute-start | bytes 49160 | tf_op jit(solution)/shard_map/ppermute | solution.py:323
  126.5 6.4 %copy-start.10 = (bf16[4,2048]{1,0:T(4,128)(2,1)}, bf16[4,2048]{1,0:T(4,128)(2,1)S(1)}, u32[]{:S(2)}) copy-start(bf16[4,2048]{1,0:T(4,128)(2,1)S(1)} %collective-permute-done.13.refs_6_) | copy-start | bytes 49156
  126.5 6.4 %collective-permute-start.18 = (bf16[4,2048]{1,0:T(4,128)(2,1)S(1)}, bf16[4,2048]{1,0:T(4,128)(2,1)S(1)}, u32[]{:S(2)}, u32[]{:S(2)}) collective-permute-start(bf16[4,2048]{1,0:T(4,128)(2,1)S(1)} %pad_maximum_fusion.refs_4_), channel_id=1, source_target_pairs={{0,28},{4,24},{8,20},{12,16},{16,12},{20,8},{24,4},{28,0},{1,29},{... | collective-permute-start | bytes 49160 | tf_op jit(solution)/shard_map/ppermute | solution.py:323
  127.9 5.0 %copy-start.11 = (bf16[4,2048]{1,0:T(4,128)(2,1)}, bf16[4,2048]{1,0:T(4,128)(2,1)S(1)}, u32[]{:S(2)}) copy-start(bf16[4,2048]{1,0:T(4,128)(2,1)S(1)} %collective-permute-done.14.refs_7_) | copy-start | bytes 49156
  128.0 5.0 %copy-start.12 = (bf16[4,2048]{1,0:T(4,128)(2,1)}, bf16[4,2048]{1,0:T(4,128)(2,1)S(1)}, u32[]{:S(2)}) copy-start(bf16[4,2048]{1,0:T(4,128)(2,1)S(1)} %collective-permute-done.15.refs_8_) | copy-start | bytes 49156
  128.0 5.0 %copy-start.13 = (bf16[4,2048]{1,0:T(4,128)(2,1)}, bf16[4,2048]{1,0:T(4,128)(2,1)S(1)}, u32[]{:S(2)}) copy-start(bf16[4,2048]{1,0:T(4,128)(2,1)S(1)} %collective-permute-done.16.refs_9_) | copy-start | bytes 49156
  128.4 4.5 %copy-start.14 = (bf16[4,2048]{1,0:T(4,128)(2,1)}, bf16[4,2048]{1,0:T(4,128)(2,1)S(1)}, u32[]{:S(2)}) copy-start(bf16[4,2048]{1,0:T(4,128)(2,1)S(1)} %collective-permute-done.17.refs_10_) | copy-start | bytes 49156
  132.9 0.6 copy-start.15
  137.0 1.9 %collective-permute-start.19 = (f32[32,128]{1,0:T(8,128)}, f32[32,128]{1,0:T(8,128)S(1)}, u32[]{:S(2)}, u32[]{:S(2)}) collective-permute-start(f32[32,128]{1,0:T(8,128)} %score.1.refs_1_), channel_id=1, source_target_pairs={{0,1},{1,0},{2,3},{3,2},{4,5},{5,4},{6,7},{7,6},{8,9},{9,8},{10,11... | collective-permute-start | bytes 49160 | tf_op jit(solution)/shard_map/ppermute | solution.py:323
  137.0 4.1 %collective-permute-start.20 = (f32[32,128]{1,0:T(8,128)}, f32[32,128]{1,0:T(8,128)S(1)}, u32[]{:S(2)}, u32[]{:S(2)}) collective-permute-start(f32[32,128]{1,0:T(8,128)} %score.1.refs_1_), channel_id=1, source_target_pairs={{0,2},{1,3},{2,0},{3,1},{4,6},{5,7},{6,4},{7,5},{8,10},{9,11},{10,... | collective-permute-start | bytes 49160 | tf_op jit(solution)/shard_map/ppermute | solution.py:323
  137.5 3.5 %collective-permute-start.21 = (f32[32,128]{1,0:T(8,128)}, f32[32,128]{1,0:T(8,128)S(1)}, u32[]{:S(2)}, u32[]{:S(2)}) collective-permute-start(f32[32,128]{1,0:T(8,128)} %score.1.refs_1_), channel_id=1, source_target_pairs={{0,3},{1,2},{2,1},{3,0},{4,7},{5,6},{6,5},{7,4},{8,11},{9,10},{10,... | collective-permute-start | bytes 49160 | tf_op jit(solution)/shard_map/ppermute | solution.py:323
  138.8 2.3 %copy-start.23 = (f32[32,128]{1,0:T(8,128)}, f32[32,128]{1,0:T(8,128)S(1)}, u32[]{:S(2)}) copy-start(f32[32,128]{1,0:T(8,128)S(1)} %collective-permute-done.19.refs_2_) | copy-start | bytes 49156
  141.1 0.6 copy-start.24
  141.7 0.6 copy-start.25
  143.8 6.4 %collective-permute-start.22 = (f32[32,128]{1,0:T(8,128)}, f32[32,128]{1,0:T(8,128)S(1)}, u32[]{:S(2)}, u32[]{:S(2)}) collective-permute-start(f32[32,128]{1,0:T(8,128)} %combine.2.refs_1_), channel_id=1, source_target_pairs={{0,4},{4,0},{8,12},{12,8},{16,20},{20,16},{24,28},{28,24},{1,5},{5... | collective-permute-start | bytes 49160 | tf_op jit(solution)/shard_map/ppermute | solution.py:323
  144.4 6.0 %collective-permute-start.23 = (f32[32,128]{1,0:T(8,128)}, f32[32,128]{1,0:T(8,128)S(1)}, u32[]{:S(2)}, u32[]{:S(2)}) collective-permute-start(f32[32,128]{1,0:T(8,128)} %combine.2.refs_1_), channel_id=1, source_target_pairs={{0,8},{4,12},{8,0},{12,4},{16,24},{20,28},{24,16},{28,20},{1,9},{5... | collective-permute-start | bytes 49160 | tf_op jit(solution)/shard_map/ppermute | solution.py:323
  144.4 10.6 %collective-permute-start.24 = (f32[32,128]{1,0:T(8,128)}, f32[32,128]{1,0:T(8,128)S(1)}, u32[]{:S(2)}, u32[]{:S(2)}) collective-permute-start(f32[32,128]{1,0:T(8,128)} %combine.2.refs_1_), channel_id=1, source_target_pairs={{0,12},{4,8},{8,4},{12,0},{16,28},{20,24},{24,20},{28,16},{1,13},{... | collective-permute-start | bytes 49160 | tf_op jit(solution)/shard_map/ppermute | solution.py:323
  147.3 7.7 %collective-permute-start.25 = (f32[32,128]{1,0:T(8,128)}, f32[32,128]{1,0:T(8,128)S(1)}, u32[]{:S(2)}, u32[]{:S(2)}) collective-permute-start(f32[32,128]{1,0:T(8,128)} %combine.2.refs_1_), channel_id=1, source_target_pairs={{0,16},{4,20},{8,24},{12,28},{16,0},{20,4},{24,8},{28,12},{1,17},{... | collective-permute-start | bytes 49160 | tf_op jit(solution)/shard_map/ppermute | solution.py:323
  147.3 7.7 %collective-permute-start.26 = (f32[32,128]{1,0:T(8,128)}, f32[32,128]{1,0:T(8,128)S(1)}, u32[]{:S(2)}, u32[]{:S(2)}) collective-permute-start(f32[32,128]{1,0:T(8,128)} %combine.2.refs_1_), channel_id=1, source_target_pairs={{0,20},{4,16},{8,28},{12,24},{16,4},{20,0},{24,12},{28,8},{1,21},{... | collective-permute-start | bytes 49160 | tf_op jit(solution)/shard_map/ppermute | solution.py:323
  150.3 6.8 %copy-start.16 = (f32[32,128]{1,0:T(8,128)}, f32[32,128]{1,0:T(8,128)S(1)}, u32[]{:S(2)}) copy-start(f32[32,128]{1,0:T(8,128)S(1)} %collective-permute-done.22.refs_2_) | copy-start | bytes 49156
  150.3 5.7 %collective-permute-start.27 = (f32[32,128]{1,0:T(8,128)}, f32[32,128]{1,0:T(8,128)S(1)}, u32[]{:S(2)}, u32[]{:S(2)}) collective-permute-start(f32[32,128]{1,0:T(8,128)} %combine.2.refs_1_), channel_id=1, source_target_pairs={{0,24},{4,28},{8,16},{12,20},{16,8},{20,12},{24,0},{28,4},{1,25},{... | collective-permute-start | bytes 49160 | tf_op jit(solution)/shard_map/ppermute | solution.py:323
  150.5 6.7 %copy-start.17 = (f32[32,128]{1,0:T(8,128)}, f32[32,128]{1,0:T(8,128)S(1)}, u32[]{:S(2)}) copy-start(f32[32,128]{1,0:T(8,128)S(1)} %collective-permute-done.23.refs_3_) | copy-start | bytes 49156
  150.5 6.6 %collective-permute-start.28 = (f32[32,128]{1,0:T(8,128)}, f32[32,128]{1,0:T(8,128)S(1)}, u32[]{:S(2)}, u32[]{:S(2)}) collective-permute-start(f32[32,128]{1,0:T(8,128)} %combine.2.refs_1_), channel_id=1, source_target_pairs={{0,28},{4,24},{8,20},{12,16},{16,12},{20,8},{24,4},{28,0},{1,29},{... | collective-permute-start | bytes 49160 | tf_op jit(solution)/shard_map/ppermute | solution.py:323
  155.0 2.1 %copy-start.18 = (f32[32,128]{1,0:T(8,128)}, f32[32,128]{1,0:T(8,128)S(1)}, u32[]{:S(2)}) copy-start(f32[32,128]{1,0:T(8,128)S(1)} %collective-permute-done.24.refs_4_) | copy-start | bytes 49156
  155.0 2.1 %copy-start.19 = (f32[32,128]{1,0:T(8,128)}, f32[32,128]{1,0:T(8,128)S(1)}, u32[]{:S(2)}) copy-start(f32[32,128]{1,0:T(8,128)S(1)} %collective-permute-done.25.refs_5_) | copy-start | bytes 49156
  155.0 2.1 %copy-start.20 = (f32[32,128]{1,0:T(8,128)}, f32[32,128]{1,0:T(8,128)S(1)}, u32[]{:S(2)}) copy-start(f32[32,128]{1,0:T(8,128)S(1)} %collective-permute-done.26.refs_6_) | copy-start | bytes 49156
  156.0 1.1 copy-start.21
  157.2 0.6 copy-start.22
where the time goes:
time: 162 us; the launch traced here: 161 us
  Pallas kernels  59.1 us (36%)
  waiting for transfers between devices  55 us (34%)
  starting transfers between devices  33.1 us (20%)
  local copies, waits for them, and re-layouts  12.2 us (8%)
    ppermute x29, waiting for transfers between devices, swap(): return lax.ppermute(array, axis, [(i, i ^ k) for i in range(size)])  55 us
    pallas_call x1, Pallas kernels, mixer(): pl.pallas_call(lambda *refs: mixer_kernel(head_count, *refs), grid=(local...  49.8 us
    ppermute x29, starting transfers between devices, swap(): return lax.ppermute(array, axis, [(i, i ^ k) for i in range(size)])  33.1 us
    unnamed x55, local copies, waits for them, and re-layouts  8.45 us
    pallas_call x1, Pallas kernels, score(): pl.pallas_call(lambda *refs: score_kernel(len(rows), head_count, *refs),...  3.45 us
    pallas_call x2, Pallas kernels, combine(): pl.pallas_call(lambda *refs: combine_kernel(finish, *refs), in_specs=[pl....  3.32 us
  transfers between devices with their start and end apart: 29, of which 12 were waited for; matrix products, arithmetic and copies ran while one was open for 3% of the time, Pallas kernels for 0%

commit v1 on v0

--- a/solution.py
+++ b/solution.py
@@ -336,18 +336,18 @@
 def score_kernel(batch_count, head_count, *refs):
     index_ref, next_ref, gain_ref, table_ref = refs[:4]
     row_refs = refs[4 : 4 + batch_count]
-    stats_ref, everyone_ref = refs[4 + batch_count :]
+    stats_ref, placed_ref, everyone_ref = refs[4 + batch_count :]
     sequences, model_width = row_refs[0].shape
     width = model_width // head_count
     for m in range(batch_count):
         rows = row_refs[m][...].astype(jnp.float32)
-        at = (index_ref[0] ^ m) * sequences
         for k in range(head_count):
-            to = pl.multiple_of((index_ref[1] ^ k) * width, width)
-            for r in range(sequences):
-                everyone_ref[pl.ds(at + r, 1), pl.ds(to, width)] = rows[
-                    r : r + 1, k * width : (k + 1) * width
-                ]
+            placed_ref[index_ref[0] ^ m, index_ref[1] ^ k] = rows[:, k * width : (k + 1) * width]
+    for m in range(batch_count):
+        for k in range(head_count):
+            everyone_ref[
+                m * sequences : (m + 1) * sequences, k * width : (k + 1) * width
+            ] = placed_ref[m, k]
     wide = everyone_ref[...]
     factor = lax.rsqrt(jnp.mean(wide * wide, axis=1, keepdims=True) + ROW_EPSILON)
     hidden = (wide * factor * gain_ref[...]).astype(jnp.bfloat16)
@@ -368,7 +368,13 @@
         in_specs=[pl.BlockSpec(memory_space=pltpu.SMEM)] + [vmem] * (3 + len(rows)),
         out_specs=vmem,
         out_shape=jax.ShapeDtypeStruct((everyone[0], HEAD_DIM), jnp.float32),
-        scratch_shapes=[pltpu.VMEM(everyone, jnp.float32)],
+        scratch_shapes=[
+            pltpu.VMEM(
+                (len(rows), head_count, rows[0].shape[0], rows[0].shape[1] // head_count),
+                jnp.float32,
+            ),
+            pltpu.VMEM(everyone, jnp.float32),
+        ],
         name="score",
     )(index, next_token[:, None], final_gain[None, :], vocab_table, *rows)
 

time: 162 us -> 161 us (level)
  no operation moved by 1% of the time
where the time goes in v1:
time: 161 us
  Pallas kernels  59 us (37%)
  waiting for transfers between devices  55 us (34%)
  starting transfers between devices  33.1 us (21%)
  local copies, waits for them, and re-layouts  12.2 us (8%)
    ppermute x29, waiting for transfers between devices, swap(): return lax.ppermute(array, axis, [(i, i ^ k) for i in range(size)])  55 us
    pallas_call x1, Pallas kernels, mixer(): pl.pallas_call(lambda *refs: mixer_kernel(head_count, *refs), grid=(local...  49.8 us
    ppermute x29, starting transfers between devices, swap(): return lax.ppermute(array, axis, [(i, i ^ k) for i in range(size)])  33.1 us
    unnamed x55, local copies, waits for them, and re-layouts  8.45 us
    pallas_call x1, Pallas kernels, score(): pl.pallas_call(lambda *refs: score_kernel(len(rows), head_count, *refs),...  3.33 us
    pallas_call x2, Pallas kernels, combine(): pl.pallas_call(lambda *refs: combine_kernel(finish, *refs), in_specs=[pl....  3.32 us
  transfers between devices with their start and end apart: 29, of which 12 were waited for; matrix products, arithmetic and copies ran while one was open for 3% of the time, Pallas kernels for 0%

profile of v1, /device:TPU:0, one launch (start us, length us, event | category | flops | bytes accessed | tf_op | source)
XLA Modules:
  0.0 160.8 jit_solution(18024916482726433793)
XLA Ops:
  0.6 3.1 %collective-permute-start.1 = (bf16[512,512]{1,0:T(8,128)(2,1)}, bf16[512,512]{1,0:T(8,128)(2,1)S(1)}, u32[]{:S(2)}, u32[]{:S(2)}) collective-permute-start(bf16[512,512]{1,0:T(8,128)(2,1)} %refs_9_.2), channel_id=1, source_target_pairs={{0,2},{1,3},{2,0},{3,1},{4,6},{5,7},{6,4},{7,5},{8,10},{9,11},{10,... | collective-permute-start | bytes 1572872 | tf_op jit(solution)/shard_map/ppermute | solution.py:323
  3.7 0.0 collective-permute-start
  3.7 12.1 %collective-permute-done.1.refs_5_ = bf16[512,512]{1,0:T(8,128)(2,1)S(1)} collective-permute-done((bf16[512,512]{1,0:T(8,128)(2,1)}, bf16[512,512]{1,0:T(8,128)(2,1)S(1)}, u32[]{:S(2)}, u32[]{:S(2)}) %collective-permute-start.1) | collective-permute-done | bytes 524320 | tf_op jit(solution)/shard_map/ppermute | solution.py:323
  15.8 0.0 collective-permute-start.2
  15.8 1.1 copy.17.refs_9_
  16.9 0.0 collective-permute-done.refs_4_
  17.0 0.8 collective-permute-done.2.refs_6_
  17.7 1.0 copy-done
  18.8 0.7 copy-done.2
  19.4 1.2 copy-done.4
  20.7 0.7 copy-done.5
  21.4 0.7 copy-done.6
  22.0 0.7 copy-done.7
  22.7 49.8 %mixer.1 = (bf16[512,512]{1,0:T(8,128)(2,1)S(1)}, f32[4,4,128,128]{3,2,1,0:T(8,128)}) custom-call(s32[1]{0:T(128)} %bitcast.refs_0_, s32[4]{0:T(128)S(1)} %copy-done.2, f32[4]{0:T(128)S(1)} %copy-done.6, bf16[512,512]{1,0:T(8,128)(2,1)S(1)} %copy-done, bf16[512,512]{1,0:T(8,128)(2,1)S(1)} %collective-permute-done.refs_4_, ...), custom_call_target="tpu_custom_call" | custom-call | flops 22548578304 | bytes 14680064 | tf_op jit(solution)/shard_map/mixer/pallas_call | solution.py:236
  72.4 1.7 %collective-permute-start.4 = (bf16[512,512]{1,0:T(8,128)(2,1)S(1)}, bf16[512,512]{1,0:T(8,128)(2,1)S(1)}, u32[]{:S(2)}, u32[]{:S(2)}) collective-permute-start(bf16[512,512]{1,0:T(8,128)(2,1)S(1)} %get-tuple-element.16.refs_1_), channel_id=1, source_target_pairs={{0,2},{1,3},{2,0},{3,1},{4,6},{5,7},{6,4},{7,5},{8,10},{9,11},{10,... | collective-permute-start | bytes 1572872 | tf_op jit(solution)/shard_map/ppermute | solution.py:323
  74.2 0.0 collective-permute-start.3
  74.2 1.7 %constant_dynamic-slice_fusion = (bf16[512,512]{1,0:T(8,128)(2,1)S(1)}, bf16[512,512]{1,0:T(8,128)(2,1)S(1)}, bf16[512,512]{1,0:T(8,128)(2,1)S(1)}, bf16[512,512]{1,0:T(8,128)(2,1)S(1)}) fusion(bf16[512,2048]{1,0:T(8,128)(2,1)} %param.20, s32[]{:T(128)S(6)} %select_n.15, s32[]{:T(128)S(6)} %select_n.14, s32[]{:T(128)S(6)} %select_n.13, s32[]{:T(128)S(6)} %select_n.12), kind=kLoop, calls=%fused_computation.2 | loop fusion | bytes 4194320 | tf_op jit(solution)/shard_map/dynamic_slice | solution.py:441
  75.9 0.5 collective-permute-start.6
  76.4 0.3 collective-permute-start.7
  76.7 1.1 collective-permute-start.8
  77.9 9.4 %collective-permute-done.4.refs_3_ = bf16[512,512]{1,0:T(8,128)(2,1)S(1)} collective-permute-done((bf16[512,512]{1,0:T(8,128)(2,1)S(1)}, bf16[512,512]{1,0:T(8,128)(2,1)S(1)}, u32[]{:S(2)}, u32[]{:S(2)}) %collective-permute-start.4) | collective-permute-done | bytes 524320 | tf_op jit(solution)/shard_map/ppermute | solution.py:323
  87.2 0.0 collective-permute-done.6.refs_6_
  87.2 11.2 %collective-permute-done.7.refs_7_ = bf16[512,512]{1,0:T(8,128)(2,1)S(1)} collective-permute-done((bf16[512,512]{1,0:T(8,128)(2,1)S(1)}, bf16[512,512]{1,0:T(8,128)(2,1)S(1)}, u32[]{:S(2)}, u32[]{:S(2)}) %collective-permute-start.7) | collective-permute-done | bytes 524320 | tf_op jit(solution)/shard_map/ppermute | solution.py:323
  98.5 9.7 %collective-permute-done.8.refs_8_ = bf16[512,512]{1,0:T(8,128)(2,1)S(1)} collective-permute-done((bf16[512,512]{1,0:T(8,128)(2,1)S(1)}, bf16[512,512]{1,0:T(8,128)(2,1)S(1)}, u32[]{:S(2)}, u32[]{:S(2)}) %collective-permute-start.8) | collective-permute-done | bytes 524320 | tf_op jit(solution)/shard_map/ppermute | solution.py:323
  108.1 0.0 collective-permute-done.3.refs_2_
  108.1 0.0 collective-permute-done.5.refs_4_
  108.2 0.0 copy-start.26
  108.2 2.6 %project.1 = (bf16[512,512]{1,0:T(8,128)(2,1)}, f32[4,512]{1,0:T(4,128)S(1)}) custom-call(s32[4]{0:T(128)S(1)} %copy-done.3, bf16[512,512]{1,0:T(8,128)(2,1)S(1)} %get-tuple-element.16.refs_1_, bf16[512,512]{1,0:T(8,128)(2,1)S(1)} %collective-permute-done.3.refs_2_, bf16[512,512]{1,0:T(8,128)(2,1)S(1)} %collective-permute-done.4.refs_3_, ...), custom_call_target="tpu_custom_call" | custom-call | tf_op jit(solution)/shard_map/project/pallas_call | solution.py:307
  110.8 1.6 %collective-permute-start.10 = (bf16[4,512]{1,0:T(4,128)(2,1)S(1)}, bf16[4,512]{1,0:T(4,128)(2,1)S(1)}, u32[]{:S(2)}, u32[]{:S(2)}) collective-permute-start(bf16[4,512]{1,0:T(4,128)(2,1)S(1)} %convert_element_type.3), channel_id=1, source_target_pairs={{0,2},{1,3},{2,0},{3,1},{4,6},{5,7},{6,4},{7,5},{8,10},{9,11},{10,... | collective-permute-start | bytes 12296 | tf_op jit(solution)/shard_map/ppermute | solution.py:323
  112.4 0.3 collective-permute-start.11
  112.7 0.2 collective-permute-start.9
  112.9 1.5 collective-permute-done.10
  114.4 1.1 collective-permute-done.11
  115.4 0.0 collective-permute-done.9
  115.5 1.6 collective-permute-start.12
  117.0 1.6 collective-permute-start.13
  118.6 0.4 collective-permute-start.14
  119.0 2.6 %collective-permute-start.15 = (bf16[4,2048]{1,0:T(4,128)(2,1)S(1)}, bf16[4,2048]{1,0:T(4,128)(2,1)S(1)}, u32[]{:S(2)}, u32[]{:S(2)}) collective-permute-start(bf16[4,2048]{1,0:T(4,128)(2,1)S(1)} %pad_maximum_fusion.refs_4_), channel_id=1, source_target_pairs={{0,16},{4,20},{8,24},{12,28},{16,0},{20,4},{24,8},{28,12},{1,17},{... | collective-permute-start | bytes 49160 | tf_op jit(solution)/shard_map/ppermute | solution.py:323
  121.6 1.3 collective-permute-start.16
  122.9 3.6 %collective-permute-start.17 = (bf16[4,2048]{1,0:T(4,128)(2,1)S(1)}, bf16[4,2048]{1,0:T(4,128)(2,1)S(1)}, u32[]{:S(2)}, u32[]{:S(2)}) collective-permute-start(bf16[4,2048]{1,0:T(4,128)(2,1)S(1)} %pad_maximum_fusion.refs_4_), channel_id=1, source_target_pairs={{0,24},{4,28},{8,16},{12,20},{16,8},{20,12},{24,0},{28,4},{1,25},{... | collective-permute-start | bytes 49160 | tf_op jit(solution)/shard_map/ppermute | solution.py:323
  126.5 0.2 collective-permute-start.18
  126.7 0.6 pad_add_fusion.refs_0_
  127.2 0.7 copy.18.refs_1_
  128.0 0.4 collective-permute-done.17.refs_10_
  128.4 4.5 %collective-permute-done.18.refs_11_ = bf16[4,2048]{1,0:T(4,128)(2,1)S(1)} collective-permute-done((bf16[4,2048]{1,0:T(4,128)(2,1)S(1)}, bf16[4,2048]{1,0:T(4,128)(2,1)S(1)}, u32[]{:S(2)}, u32[]{:S(2)}) %collective-permute-start.18) | collective-permute-done | bytes 16416 | tf_op jit(solution)/shard_map/ppermute | solution.py:323
  133.0 0.5 copy-done.15
  133.5 3.3 %score.1.refs_1_ = f32[32,128]{1,0:T(8,128)} custom-call(s32[3]{0:T(128)} %pad_add_fusion.refs_0_, s32[32,1]{1,0:T(8,128)} %copy.18.refs_1_, f32[1,2048]{1,0:T(1,128)} %bitcast.9, bf16[512,2048]{1,0:T(8,128)(2,1)} %refs_3_.2, bf16[4,2048]{1,0:T(4,128)(2,1)} %copy-done.8, bf16[4,2048]{1,0:T(4,128)(2,1)} %copy-done.9, bf16[4,2048]{1,0:T(4,128)(2,1)} %copy-done.10, ...), custom_call_target="tpu_custom_call" | custom-call | tf_op jit(solution)/shard_map/score/pallas_call | solution.py:366
  136.8 0.6 collective-permute-start.20
  137.4 1.3 collective-permute-start.21
  138.7 2.3 %collective-permute-done.20.refs_3_ = f32[32,128]{1,0:T(8,128)S(1)} collective-permute-done((f32[32,128]{1,0:T(8,128)}, f32[32,128]{1,0:T(8,128)S(1)}, u32[]{:S(2)}, u32[]{:S(2)}) %collective-permute-start.20) | collective-permute-done | bytes 16416 | tf_op jit(solution)/shard_map/ppermute | solution.py:323
  141.0 0.0 collective-permute-done.21.refs_4_
  141.0 0.6 copy-done.24
  141.6 0.6 copy-done.25
  142.2 1.5 combine.2.refs_1_
  143.7 0.6 collective-permute-start.22
  144.3 2.9 %collective-permute-start.24 = (f32[32,128]{1,0:T(8,128)}, f32[32,128]{1,0:T(8,128)S(1)}, u32[]{:S(2)}, u32[]{:S(2)}) collective-permute-start(f32[32,128]{1,0:T(8,128)} %combine.2.refs_1_), channel_id=1, source_target_pairs={{0,12},{4,8},{8,4},{12,0},{16,28},{20,24},{24,20},{28,16},{1,13},{... | collective-permute-start | bytes 49160 | tf_op jit(solution)/shard_map/ppermute | solution.py:323
  147.2 2.9 %collective-permute-start.26 = (f32[32,128]{1,0:T(8,128)}, f32[32,128]{1,0:T(8,128)S(1)}, u32[]{:S(2)}, u32[]{:S(2)}) collective-permute-start(f32[32,128]{1,0:T(8,128)} %combine.2.refs_1_), channel_id=1, source_target_pairs={{0,20},{4,16},{8,28},{12,24},{16,4},{20,0},{24,12},{28,8},{1,21},{... | collective-permute-start | bytes 49160 | tf_op jit(solution)/shard_map/ppermute | solution.py:323
  150.2 0.2 collective-permute-start.27
  150.4 4.5 %collective-permute-start.28 = (f32[32,128]{1,0:T(8,128)}, f32[32,128]{1,0:T(8,128)S(1)}, u32[]{:S(2)}, u32[]{:S(2)}) collective-permute-start(f32[32,128]{1,0:T(8,128)} %combine.2.refs_1_), channel_id=1, source_target_pairs={{0,28},{4,24},{8,20},{12,16},{16,12},{20,8},{24,4},{28,0},{1,29},{... | collective-permute-start | bytes 49160 | tf_op jit(solution)/shard_map/ppermute | solution.py:323
  154.9 1.0 collective-permute-done.27.refs_7_
  155.9 1.1 collective-permute-done.28.refs_8_
  157.0 0.6 copy-done.22
  157.6 1.8 %combine.3 = f32[32,128]{1,0:T(8,128)} custom-call(s32[1]{0:T(128)} %bitcast.3.refs_0_, f32[32,128]{1,0:T(8,128)} %combine.2.refs_1_, f32[32,128]{1,0:T(8,128)} %copy-done.16, f32[32,128]{1,0:T(8,128)} %copy-done.17, f32[32,128]{1,0:T(8,128)} %copy-done.18, f32[32,128]{1,0:T(8,128)} %copy-done.19, f32[32,128]{1,0:T(8,128)} %copy-done.20, ...), custom_call_target="tpu_custom_call" | custom-call | tf_op jit(solution)/shard_map/combine/pallas_call | solution.py:404
  159.4 1.3 slice_reduce_fusion
  (60 shorter events, 0.1 us)
Async XLA Ops:
  0.6 15.2 %collective-permute-start.1 = (bf16[512,512]{1,0:T(8,128)(2,1)}, bf16[512,512]{1,0:T(8,128)(2,1)S(1)}, u32[]{:S(2)}, u32[]{:S(2)}) collective-permute-start(bf16[512,512]{1,0:T(8,128)(2,1)} %refs_9_.2), channel_id=1, source_target_pairs={{0,2},{1,3},{2,0},{3,1},{4,6},{5,7},{6,4},{7,5},{8,10},{9,11},{10,... | collective-permute-start | bytes 1572872 | tf_op jit(solution)/shard_map/ppermute | solution.py:323
  3.7 13.3 %collective-permute-start = (bf16[512,512]{1,0:T(8,128)(2,1)}, bf16[512,512]{1,0:T(8,128)(2,1)S(1)}, u32[]{:S(2)}, u32[]{:S(2)}) collective-permute-start(bf16[512,512]{1,0:T(8,128)(2,1)} %refs_9_.2), channel_id=1, source_target_pairs={{0,1},{1,0},{2,3},{3,2},{4,5},{5,4},{6,7},{7,6},{8,9},{9,8},{10,11... | collective-permute-start | bytes 1572872 | tf_op jit(solution)/shard_map/ppermute | solution.py:323
  15.8 1.9 %collective-permute-start.2 = (bf16[512,512]{1,0:T(8,128)(2,1)S(1)}, bf16[512,512]{1,0:T(8,128)(2,1)S(1)}, u32[]{:S(2)}, u32[]{:S(2)}) collective-permute-start(bf16[512,512]{1,0:T(8,128)(2,1)S(1)} %collective-permute-done.1.refs_5_), channel_id=1, source_target_pairs={{0,1},{1,0},{2,3},{3,2},{4,5},{5,4},{6,7},{7,6},{8,9},{9,8},{10,11... | collective-permute-start | bytes 1572872 | tf_op jit(solution)/shard_map/ppermute | solution.py:323
  17.7 1.0 copy-start
  18.8 0.7 copy-start.2
  19.4 1.2 copy-start.4
  20.7 0.7 copy-start.5
  21.4 0.7 copy-start.6
  22.0 0.7 copy-start.7
  72.4 14.8 %collective-permute-start.4 = (bf16[512,512]{1,0:T(8,128)(2,1)S(1)}, bf16[512,512]{1,0:T(8,128)(2,1)S(1)}, u32[]{:S(2)}, u32[]{:S(2)}) collective-permute-start(bf16[512,512]{1,0:T(8,128)(2,1)S(1)} %get-tuple-element.16.refs_1_), channel_id=1, source_target_pairs={{0,2},{1,3},{2,0},{3,1},{4,6},{5,7},{6,4},{7,5},{8,10},{9,11},{10,... | collective-permute-start | bytes 1572872 | tf_op jit(solution)/shard_map/ppermute | solution.py:323
  74.2 34.0 %copy-start.1 = (bf16[512,512]{1,0:T(8,128)(2,1)S(1)}, bf16[512,512]{1,0:T(8,128)(2,1)}, u32[]{:S(2)}) copy-start(bf16[512,512]{1,0:T(8,128)(2,1)} %refs_9_.2) | copy-start | bytes 1572868
  74.2 34.0 %copy-start.3 = (s32[4]{0:T(128)S(1)}, s32[4]{0:T(128)}, u32[]{:S(2)}) copy-start(s32[4]{0:T(128)} %refs_0_.1) | copy-start | bytes 52
  74.2 33.9 %collective-permute-start.3 = (bf16[512,512]{1,0:T(8,128)(2,1)S(1)}, bf16[512,512]{1,0:T(8,128)(2,1)S(1)}, u32[]{:S(2)}, u32[]{:S(2)}) collective-permute-start(bf16[512,512]{1,0:T(8,128)(2,1)S(1)} %get-tuple-element.16.refs_1_), channel_id=1, source_target_pairs={{0,1},{1,0},{2,3},{3,2},{4,5},{5,4},{6,7},{7,6},{8,9},{9,8},{10,11... | collective-permute-start | bytes 1572872 | tf_op jit(solution)/shard_map/ppermute | solution.py:323
  75.9 11.3 %collective-permute-start.6 = (bf16[512,512]{1,0:T(8,128)(2,1)S(1)}, bf16[512,512]{1,0:T(8,128)(2,1)S(1)}, u32[]{:S(2)}, u32[]{:S(2)}) collective-permute-start(bf16[512,512]{1,0:T(8,128)(2,1)S(1)} %get-tuple-element.23), channel_id=1, source_target_pairs={{0,1},{1,0},{2,3},{3,2},{4,5},{5,4},{6,7},{7,6},{8,9},{9,8},{10,11... | collective-permute-start | bytes 1572872 | tf_op jit(solution)/shard_map/ppermute | solution.py:323
  76.4 22.0 %collective-permute-start.7 = (bf16[512,512]{1,0:T(8,128)(2,1)S(1)}, bf16[512,512]{1,0:T(8,128)(2,1)S(1)}, u32[]{:S(2)}, u32[]{:S(2)}) collective-permute-start(bf16[512,512]{1,0:T(8,128)(2,1)S(1)} %get-tuple-element.22), channel_id=1, source_target_pairs={{0,2},{1,3},{2,0},{3,1},{4,6},{5,7},{6,4},{7,5},{8,10},{9,11},{10,... | collective-permute-start | bytes 1572872 | tf_op jit(solution)/shard_map/ppermute | solution.py:323
  76.7 31.4 %collective-permute-start.8 = (bf16[512,512]{1,0:T(8,128)(2,1)S(1)}, bf16[512,512]{1,0:T(8,128)(2,1)S(1)}, u32[]{:S(2)}, u32[]{:S(2)}) collective-permute-start(bf16[512,512]{1,0:T(8,128)(2,1)S(1)} %get-tuple-element.21), channel_id=1, source_target_pairs={{0,3},{1,2},{2,1},{3,0},{4,7},{5,6},{6,5},{7,4},{8,11},{9,10},{10,... | collective-permute-start | bytes 1572872 | tf_op jit(solution)/shard_map/ppermute | solution.py:323
  87.2 20.9 %collective-permute-start.5 = (bf16[512,512]{1,0:T(8,128)(2,1)S(1)}, bf16[512,512]{1,0:T(8,128)(2,1)S(1)}, u32[]{:S(2)}, u32[]{:S(2)}) collective-permute-start(bf16[512,512]{1,0:T(8,128)(2,1)S(1)} %collective-permute-done.4.refs_3_), channel_id=1, source_target_pairs={{0,1},{1,0},{2,3},{3,2},{4,5},{5,4},{6,7},{7,6},{8,9},{9,8},{10,11... | collective-permute-start | bytes 1572872 | tf_op jit(solution)/shard_map/ppermute | solution.py:323
  108.2 19.1 %copy-start.26 = (s32[32]{0:T(128)S(1)}, s32[32]{0:T(128)}, u32[]{:S(2)}) copy-start(s32[32]{0:T(128)} %param.23) | copy-start | bytes 388
  110.8 3.6 %collective-permute-start.10 = (bf16[4,512]{1,0:T(4,128)(2,1)S(1)}, bf16[4,512]{1,0:T(4,128)(2,1)S(1)}, u32[]{:S(2)}, u32[]{:S(2)}) collective-permute-start(bf16[4,512]{1,0:T(4,128)(2,1)S(1)} %convert_element_type.3), channel_id=1, source_target_pairs={{0,2},{1,3},{2,0},{3,1},{4,6},{5,7},{6,4},{7,5},{8,10},{9,11},{10,... | collective-permute-start | bytes 12296 | tf_op jit(solution)/shard_map/ppermute | solution.py:323
  112.4 3.0 %collective-permute-start.11 = (bf16[4,512]{1,0:T(4,128)(2,1)S(1)}, bf16[4,512]{1,0:T(4,128)(2,1)S(1)}, u32[]{:S(2)}, u32[]{:S(2)}) collective-permute-start(bf16[4,512]{1,0:T(4,128)(2,1)S(1)} %convert_element_type.3), channel_id=1, source_target_pairs={{0,3},{1,2},{2,1},{3,0},{4,7},{5,6},{6,5},{7,4},{8,11},{9,10},{10,... | collective-permute-start | bytes 12296 | tf_op jit(solution)/shard_map/ppermute | solution.py:323
  112.7 2.7 %collective-permute-start.9 = (bf16[4,512]{1,0:T(4,128)(2,1)S(1)}, bf16[4,512]{1,0:T(4,128)(2,1)S(1)}, u32[]{:S(2)}, u32[]{:S(2)}) collective-permute-start(bf16[4,512]{1,0:T(4,128)(2,1)S(1)} %convert_element_type.3), channel_id=1, source_target_pairs={{0,1},{1,0},{2,3},{3,2},{4,5},{5,4},{6,7},{7,6},{8,9},{9,8},{10,11... | collective-permute-start | bytes 12296 | tf_op jit(solution)/shard_map/ppermute | solution.py:323
  115.5 17.5 %copy-start.8 = (bf16[4,2048]{1,0:T(4,128)(2,1)}, bf16[4,2048]{1,0:T(4,128)(2,1)S(1)}, u32[]{:S(2)}) copy-start(bf16[4,2048]{1,0:T(4,128)(2,1)S(1)} %pad_maximum_fusion.refs_4_) | copy-start | bytes 49156
  115.5 7.4 %collective-permute-start.12 = (bf16[4,2048]{1,0:T(4,128)(2,1)S(1)}, bf16[4,2048]{1,0:T(4,128)(2,1)S(1)}, u32[]{:S(2)}, u32[]{:S(2)}) collective-permute-start(bf16[4,2048]{1,0:T(4,128)(2,1)S(1)} %pad_maximum_fusion.refs_4_), channel_id=1, source_target_pairs={{0,4},{4,0},{8,12},{12,8},{16,20},{20,16},{24,28},{28,24},{1,5},{5... | collective-permute-start | bytes 49160 | tf_op jit(solution)/shard_map/ppermute | solution.py:323
  117.0 9.4 %collective-permute-start.13 = (bf16[4,2048]{1,0:T(4,128)(2,1)S(1)}, bf16[4,2048]{1,0:T(4,128)(2,1)S(1)}, u32[]{:S(2)}, u32[]{:S(2)}) collective-permute-start(bf16[4,2048]{1,0:T(4,128)(2,1)S(1)} %pad_maximum_fusion.refs_4_), channel_id=1, source_target_pairs={{0,8},{4,12},{8,0},{12,4},{16,24},{20,28},{24,16},{28,20},{1,9},{5... | collective-permute-start | bytes 49160 | tf_op jit(solution)/shard_map/ppermute | solution.py:323
  118.6 9.3 %collective-permute-start.14 = (bf16[4,2048]{1,0:T(4,128)(2,1)S(1)}, bf16[4,2048]{1,0:T(4,128)(2,1)S(1)}, u32[]{:S(2)}, u32[]{:S(2)}) collective-permute-start(bf16[4,2048]{1,0:T(4,128)(2,1)S(1)} %pad_maximum_fusion.refs_4_), channel_id=1, source_target_pairs={{0,12},{4,8},{8,4},{12,0},{16,28},{20,24},{24,20},{28,16},{1,13},{... | collective-permute-start | bytes 49160 | tf_op jit(solution)/shard_map/ppermute | solution.py:323
  119.0 8.9 %collective-permute-start.15 = (bf16[4,2048]{1,0:T(4,128)(2,1)S(1)}, bf16[4,2048]{1,0:T(4,128)(2,1)S(1)}, u32[]{:S(2)}, u32[]{:S(2)}) collective-permute-start(bf16[4,2048]{1,0:T(4,128)(2,1)S(1)} %pad_maximum_fusion.refs_4_), channel_id=1, source_target_pairs={{0,16},{4,20},{8,24},{12,28},{16,0},{20,4},{24,8},{28,12},{1,17},{... | collective-permute-start | bytes 49160 | tf_op jit(solution)/shard_map/ppermute | solution.py:323
  121.6 6.3 %collective-permute-start.16 = (bf16[4,2048]{1,0:T(4,128)(2,1)S(1)}, bf16[4,2048]{1,0:T(4,128)(2,1)S(1)}, u32[]{:S(2)}, u32[]{:S(2)}) collective-permute-start(bf16[4,2048]{1,0:T(4,128)(2,1)S(1)} %pad_maximum_fusion.refs_4_), channel_id=1, source_target_pairs={{0,20},{4,16},{8,28},{12,24},{16,4},{20,0},{24,12},{28,8},{1,21},{... | collective-permute-start | bytes 49160 | tf_op jit(solution)/shard_map/ppermute | solution.py:323
  122.9 10.0 %copy-start.9 = (bf16[4,2048]{1,0:T(4,128)(2,1)}, bf16[4,2048]{1,0:T(4,128)(2,1)S(1)}, u32[]{:S(2)}) copy-start(bf16[4,2048]{1,0:T(4,128)(2,1)S(1)} %collective-permute-done.12.refs_5_) | copy-start | bytes 49156
  122.9 5.5 %collective-permute-start.17 = (bf16[4,2048]{1,0:T(4,128)(2,1)S(1)}, bf16[4,2048]{1,0:T(4,128)(2,1)S(1)}, u32[]{:S(2)}, u32[]{:S(2)}) collective-permute-start(bf16[4,2048]{1,0:T(4,128)(2,1)S(1)} %pad_maximum_fusion.refs_4_), channel_id=1, source_target_pairs={{0,24},{4,28},{8,16},{12,20},{16,8},{20,12},{24,0},{28,4},{1,25},{... | collective-permute-start | bytes 49160 | tf_op jit(solution)/shard_map/ppermute | solution.py:323
  126.5 6.4 %copy-start.10 = (bf16[4,2048]{1,0:T(4,128)(2,1)}, bf16[4,2048]{1,0:T(4,128)(2,1)S(1)}, u32[]{:S(2)}) copy-start(bf16[4,2048]{1,0:T(4,128)(2,1)S(1)} %collective-permute-done.13.refs_6_) | copy-start | bytes 49156
  126.5 6.4 %collective-permute-start.18 = (bf16[4,2048]{1,0:T(4,128)(2,1)S(1)}, bf16[4,2048]{1,0:T(4,128)(2,1)S(1)}, u32[]{:S(2)}, u32[]{:S(2)}) collective-permute-start(bf16[4,2048]{1,0:T(4,128)(2,1)S(1)} %pad_maximum_fusion.refs_4_), channel_id=1, source_target_pairs={{0,28},{4,24},{8,20},{12,16},{16,12},{20,8},{24,4},{28,0},{1,29},{... | collective-permute-start | bytes 49160 | tf_op jit(solution)/shard_map/ppermute | solution.py:323
  127.9 5.0 %copy-start.11 = (bf16[4,2048]{1,0:T(4,128)(2,1)}, bf16[4,2048]{1,0:T(4,128)(2,1)S(1)}, u32[]{:S(2)}) copy-start(bf16[4,2048]{1,0:T(4,128)(2,1)S(1)} %collective-permute-done.14.refs_7_) | copy-start | bytes 49156
  128.0 5.0 %copy-start.12 = (bf16[4,2048]{1,0:T(4,128)(2,1)}, bf16[4,2048]{1,0:T(4,128)(2,1)S(1)}, u32[]{:S(2)}) copy-start(bf16[4,2048]{1,0:T(4,128)(2,1)S(1)} %collective-permute-done.15.refs_8_) | copy-start | bytes 49156
  128.0 5.0 %copy-start.13 = (bf16[4,2048]{1,0:T(4,128)(2,1)}, bf16[4,2048]{1,0:T(4,128)(2,1)S(1)}, u32[]{:S(2)}) copy-start(bf16[4,2048]{1,0:T(4,128)(2,1)S(1)} %collective-permute-done.16.refs_9_) | copy-start | bytes 49156
  128.4 4.5 %copy-start.14 = (bf16[4,2048]{1,0:T(4,128)(2,1)}, bf16[4,2048]{1,0:T(4,128)(2,1)S(1)}, u32[]{:S(2)}) copy-start(bf16[4,2048]{1,0:T(4,128)(2,1)S(1)} %collective-permute-done.17.refs_10_) | copy-start | bytes 49156
  132.9 0.6 copy-start.15
  136.8 1.9 %collective-permute-start.19 = (f32[32,128]{1,0:T(8,128)}, f32[32,128]{1,0:T(8,128)S(1)}, u32[]{:S(2)}, u32[]{:S(2)}) collective-permute-start(f32[32,128]{1,0:T(8,128)} %score.1.refs_1_), channel_id=1, source_target_pairs={{0,1},{1,0},{2,3},{3,2},{4,5},{5,4},{6,7},{7,6},{8,9},{9,8},{10,11... | collective-permute-start | bytes 49160 | tf_op jit(solution)/shard_map/ppermute | solution.py:323
  136.8 4.1 %collective-permute-start.20 = (f32[32,128]{1,0:T(8,128)}, f32[32,128]{1,0:T(8,128)S(1)}, u32[]{:S(2)}, u32[]{:S(2)}) collective-permute-start(f32[32,128]{1,0:T(8,128)} %score.1.refs_1_), channel_id=1, source_target_pairs={{0,2},{1,3},{2,0},{3,1},{4,6},{5,7},{6,4},{7,5},{8,10},{9,11},{10,... | collective-permute-start | bytes 49160 | tf_op jit(solution)/shard_map/ppermute | solution.py:323
  137.4 3.5 %collective-permute-start.21 = (f32[32,128]{1,0:T(8,128)}, f32[32,128]{1,0:T(8,128)S(1)}, u32[]{:S(2)}, u32[]{:S(2)}) collective-permute-start(f32[32,128]{1,0:T(8,128)} %score.1.refs_1_), channel_id=1, source_target_pairs={{0,3},{1,2},{2,1},{3,0},{4,7},{5,6},{6,5},{7,4},{8,11},{9,10},{10,... | collective-permute-start | bytes 49160 | tf_op jit(solution)/shard_map/ppermute | solution.py:323
  138.7 2.3 %copy-start.23 = (f32[32,128]{1,0:T(8,128)}, f32[32,128]{1,0:T(8,128)S(1)}, u32[]{:S(2)}) copy-start(f32[32,128]{1,0:T(8,128)S(1)} %collective-permute-done.19.refs_2_) | copy-start | bytes 49156
  141.0 0.6 copy-start.24
  141.6 0.6 copy-start.25
  143.7 6.4 %collective-permute-start.22 = (f32[32,128]{1,0:T(8,128)}, f32[32,128]{1,0:T(8,128)S(1)}, u32[]{:S(2)}, u32[]{:S(2)}) collective-permute-start(f32[32,128]{1,0:T(8,128)} %combine.2.refs_1_), channel_id=1, source_target_pairs={{0,4},{4,0},{8,12},{12,8},{16,20},{20,16},{24,28},{28,24},{1,5},{5... | collective-permute-start | bytes 49160 | tf_op jit(solution)/shard_map/ppermute | solution.py:323
  144.3 6.0 %collective-permute-start.23 = (f32[32,128]{1,0:T(8,128)}, f32[32,128]{1,0:T(8,128)S(1)}, u32[]{:S(2)}, u32[]{:S(2)}) collective-permute-start(f32[32,128]{1,0:T(8,128)} %combine.2.refs_1_), channel_id=1, source_target_pairs={{0,8},{4,12},{8,0},{12,4},{16,24},{20,28},{24,16},{28,20},{1,9},{5... | collective-permute-start | bytes 49160 | tf_op jit(solution)/shard_map/ppermute | solution.py:323
  144.3 10.6 %collective-permute-start.24 = (f32[32,128]{1,0:T(8,128)}, f32[32,128]{1,0:T(8,128)S(1)}, u32[]{:S(2)}, u32[]{:S(2)}) collective-permute-start(f32[32,128]{1,0:T(8,128)} %combine.2.refs_1_), channel_id=1, source_target_pairs={{0,12},{4,8},{8,4},{12,0},{16,28},{20,24},{24,20},{28,16},{1,13},{... | collective-permute-start | bytes 49160 | tf_op jit(solution)/shard_map/ppermute | solution.py:323
  147.2 7.7 %collective-permute-start.25 = (f32[32,128]{1,0:T(8,128)}, f32[32,128]{1,0:T(8,128)S(1)}, u32[]{:S(2)}, u32[]{:S(2)}) collective-permute-start(f32[32,128]{1,0:T(8,128)} %combine.2.refs_1_), channel_id=1, source_target_pairs={{0,16},{4,20},{8,24},{12,28},{16,0},{20,4},{24,8},{28,12},{1,17},{... | collective-permute-start | bytes 49160 | tf_op jit(solution)/shard_map/ppermute | solution.py:323
  147.2 7.7 %collective-permute-start.26 = (f32[32,128]{1,0:T(8,128)}, f32[32,128]{1,0:T(8,128)S(1)}, u32[]{:S(2)}, u32[]{:S(2)}) collective-permute-start(f32[32,128]{1,0:T(8,128)} %combine.2.refs_1_), channel_id=1, source_target_pairs={{0,20},{4,16},{8,28},{12,24},{16,4},{20,0},{24,12},{28,8},{1,21},{... | collective-permute-start | bytes 49160 | tf_op jit(solution)/shard_map/ppermute | solution.py:323
  150.2 6.8 %copy-start.16 = (f32[32,128]{1,0:T(8,128)}, f32[32,128]{1,0:T(8,128)S(1)}, u32[]{:S(2)}) copy-start(f32[32,128]{1,0:T(8,128)S(1)} %collective-permute-done.22.refs_2_) | copy-start | bytes 49156
  150.2 5.7 %collective-permute-start.27 = (f32[32,128]{1,0:T(8,128)}, f32[32,128]{1,0:T(8,128)S(1)}, u32[]{:S(2)}, u32[]{:S(2)}) collective-permute-start(f32[32,128]{1,0:T(8,128)} %combine.2.refs_1_), channel_id=1, source_target_pairs={{0,24},{4,28},{8,16},{12,20},{16,8},{20,12},{24,0},{28,4},{1,25},{... | collective-permute-start | bytes 49160 | tf_op jit(solution)/shard_map/ppermute | solution.py:323
  150.3 6.7 %copy-start.17 = (f32[32,128]{1,0:T(8,128)}, f32[32,128]{1,0:T(8,128)S(1)}, u32[]{:S(2)}) copy-start(f32[32,128]{1,0:T(8,128)S(1)} %collective-permute-done.23.refs_3_) | copy-start | bytes 49156
  150.4 6.6 %collective-permute-start.28 = (f32[32,128]{1,0:T(8,128)}, f32[32,128]{1,0:T(8,128)S(1)}, u32[]{:S(2)}, u32[]{:S(2)}) collective-permute-start(f32[32,128]{1,0:T(8,128)} %combine.2.refs_1_), channel_id=1, source_target_pairs={{0,28},{4,24},{8,20},{12,16},{16,12},{20,8},{24,4},{28,0},{1,29},{... | collective-permute-start | bytes 49160 | tf_op jit(solution)/shard_map/ppermute | solution.py:323
  154.9 2.1 %copy-start.18 = (f32[32,128]{1,0:T(8,128)}, f32[32,128]{1,0:T(8,128)S(1)}, u32[]{:S(2)}) copy-start(f32[32,128]{1,0:T(8,128)S(1)} %collective-permute-done.24.refs_4_) | copy-start | bytes 49156
  154.9 2.1 %copy-start.19 = (f32[32,128]{1,0:T(8,128)}, f32[32,128]{1,0:T(8,128)S(1)}, u32[]{:S(2)}) copy-start(f32[32,128]{1,0:T(8,128)S(1)} %collective-permute-done.25.refs_5_) | copy-start | bytes 49156
  154.9 2.1 %copy-start.20 = (f32[32,128]{1,0:T(8,128)}, f32[32,128]{1,0:T(8,128)S(1)}, u32[]{:S(2)}) copy-start(f32[32,128]{1,0:T(8,128)S(1)} %collective-permute-done.26.refs_6_) | copy-start | bytes 49156
  155.9 1.1 copy-start.21
  157.0 0.6 copy-start.22
